TPU v7x, 32 devices: a whole 2x2x4 slice. The times are simulated.
32 devices in a mesh: grp: 4 (over z), sp: 8 (over y, x, core).
Axes of the slice: x: 2, y: 2, z: 4, core: 2. Of those that a mesh axis runs over, the one named last changes fastest.
Arguments:
- tokens: bfloat16 [2048, 2880], P(('grp', 'sp')), may hold values from -36 to 36
- query_weight: bfloat16 [2880, 2048], P(None, 'sp'), may hold values from -0.109375 to 0.109375
- key_value_weight: bfloat16 [2880, 1024], replicated, may hold values from -0.109375 to 0.109375
- block_places: int32 [16], replicated, may hold values from 0 to 15, each once
- sinks: float32 [32], replicated, may hold values from -1 to 5
Outputs:
- attended: bfloat16 [2048, 2048], P(('grp', 'sp'))
Inputs may be any that keep to these rules, and one draw needn't show every extreme that they name: `block_places`: every sequence block appears once.
All inputs are finite; a program needn't handle non-finite values.
Results may differ from a plain program's by a relative error of at most 0.008.
The roundings to bfloat16 on the way count: a program that leaves them out, or rounds other values in their place, can miss the bound.
Values may be sent and summed in bfloat16 or wider, within the bound.
A program may use at most 128 MiB of HBM per device.

v0:
```python
import functools

import jax
import jax.numpy as jnp
from jax import lax
from jax.experimental import pallas as pl
from jax.experimental.pallas import tpu as pltpu
from jax.sharding import PartitionSpec as P

QUERY_HEADS = 32
HEAD_SIZE = 64
BPG = 4
LANES = 128

rope_base = 150000.0
neg_large = -1e30


def rotate_heads(x, cosine, sine):
    width = x.shape[1]
    half = HEAD_SIZE // 2
    if width % LANES:
        swapped = jnp.concatenate([x[:, half:], x[:, :half]], axis=1)
        return x * cosine[:, :width] + swapped * sine[:, :width]
    parts = []
    lane = lax.broadcasted_iota(jnp.int32, (x.shape[0], LANES), 1)
    first = lane % HEAD_SIZE < half
    for j in range(width // LANES):
        v = x[:, j * LANES : (j + 1) * LANES]
        swapped = jnp.where(first, pltpu.roll(v, LANES - half, 1), pltpu.roll(v, half, 1))
        parts.append(v * cosine + swapped * sine)
    return parts[0] if len(parts) == 1 else jnp.concatenate(parts, axis=1)


def kernel(
    grp, sp, qheads, kv_total,
    tok, wq_any, kvw_any, inverse_ref, places_ref, sink, out,
    toks, wq, wkv, kvb, q, abuf, obuf, cos_ref, sin_ref, qpos, kpos,
    wsem, tsend, tfwd, trecv, ksend, krecv, osend, orecv,
):
    s = lax.axis_index("sp")
    g = lax.axis_index("grp")
    rows = tok.shape[0]
    group_rows = rows * sp
    chips = sp // 2
    pair = 2 * rows
    qc = qheads * HEAD_SIZE
    c = s // 2
    par = s % 2
    partner = s + 1 - 2 * par
    head = s * kv_total // sp
    hpar = head % 2
    koff = pl.multiple_of(head // 2 * LANES, LANES)
    voff = pl.multiple_of(kv_total * HEAD_SIZE + head // 2 * LANES, LANES)

    wcopies = [
        pltpu.make_async_copy(wq_any, wq, wsem.at[0]),
        pltpu.make_async_copy(
            kvw_any.at[:, pl.ds(koff, LANES)], wkv.at[:, pl.ds(0, LANES)], wsem.at[1]
        ),
        pltpu.make_async_copy(
            kvw_any.at[:, pl.ds(voff, LANES)], wkv.at[:, pl.ds(LANES, LANES)], wsem.at[2]
        ),
    ]

    def send_tok(to):
        return pltpu.make_async_remote_copy(
            src_ref=tok, dst_ref=toks.at[s], send_sem=tsend.at[to], recv_sem=trecv.at[s],
            device_id={"sp": to},
        )

    def forward(slot):
        return pltpu.make_async_remote_copy(
            src_ref=toks.at[slot], dst_ref=toks.at[slot], send_sem=tfwd.at[slot],
            recv_sem=trecv.at[slot], device_id={"sp": partner},
        )

    def send_kv(chip, d):
        span = pl.ds(pl.multiple_of(g * group_rows + chip * pair, pair), pair)
        return pltpu.make_async_remote_copy(
            src_ref=kvb.at[span], dst_ref=kvb.at[span], send_sem=ksend.at[d, chip],
            recv_sem=krecv.at[g, chip], device_id={"grp": (g + d) % grp},
        )

    def recv_kv(chip, d):
        src = (g + d) % grp
        span = pl.ds(pl.multiple_of(src * group_rows + chip * pair, pair), pair)
        return pltpu.make_async_remote_copy(
            src_ref=kvb.at[span], dst_ref=kvb.at[span], send_sem=ksend.at[d, chip],
            recv_sem=krecv.at[src, chip], device_id={"grp": src},
        )

    def send_out(to):
        return pltpu.make_async_remote_copy(
            src_ref=abuf.at[to], dst_ref=obuf.at[s], send_sem=osend.at[to],
            recv_sem=orecv.at[s], device_id={"sp": to},
        )

    def recv_out(src):
        return pltpu.make_async_remote_copy(
            src_ref=abuf.at[src], dst_ref=obuf.at[src], send_sem=osend.at[src],
            recv_sem=orecv.at[src], device_id={"sp": src},
        )

    send_tok(partner).start()

    def start_tok(k, _):
        send_tok((c + k) % chips * 2 + par).start()
        return 0

    lax.fori_loop(1, chips, start_tok, 0)
    for copy in wcopies:
        copy.start()
    toks[s] = tok[...]

    block_rows = group_rows // BPG
    for j in range(kpos.shape[1] // block_rows):
        within = lax.broadcasted_iota(jnp.int32, (1, block_rows), 1)
        kpos[:, j * block_rows : (j + 1) * block_rows] = places_ref[j] * block_rows + within
    wide = lax.broadcasted_iota(jnp.int32, (1, LANES), 1)
    half = HEAD_SIZE // 2
    inverse = inverse_ref[...]
    sign = jnp.where(wide % HEAD_SIZE < half, -1.0, 1.0)
    for j in range(BPG):
        rspan = slice(j * block_rows, (j + 1) * block_rows)
        within = lax.broadcasted_iota(jnp.int32, (block_rows, LANES), 0)
        place = places_ref[g * BPG + j] * block_rows + within
        qpos[rspan, :] = place[:, :1]
        angles = place.astype(jnp.float32) * inverse
        cos_ref[rspan, :] = jnp.cos(angles)
        sin_ref[rspan, :] = jnp.sin(angles) * sign
    for copy in wcopies:
        copy.wait()

    def project(k, _):
        chip = (c + chips - k) % chips

        @pl.when(k > 0)
        def _():
            slot = chip * 2 + par
            forward(slot).wait_recv()
            forward(slot).start()

        forward(chip * 2 + 1 - par).wait_recv()
        x = toks[pl.ds(chip * 2, 2)].reshape(pair, tok.shape[1])
        span = pl.ds(pl.multiple_of(chip * pair, pair), pair)
        cosine = cos_ref[span, :]
        sine = sin_ref[span, :]
        kv = jnp.dot(x, wkv[...], preferred_element_type=jnp.float32)
        keys = rotate_heads(kv[:, :LANES], cosine, sine)
        values = kv[:, LANES:]
        low = hpar == 0
        keys = jnp.where(low, keys, pltpu.roll(keys, HEAD_SIZE, 1))
        values = jnp.where(low, pltpu.roll(values, HEAD_SIZE, 1), values)
        lane = lax.broadcasted_iota(jnp.int32, (pair, LANES), 1)
        joined = jnp.where(lane < HEAD_SIZE, keys, values).astype(jnp.bfloat16)
        kvb[pl.ds(pl.multiple_of(g * group_rows + chip * pair, pair), pair), :] = joined
        for d in range(1, grp):
            send_kv(chip, d).start()
        qf = jnp.dot(x, wq[...], preferred_element_type=jnp.float32)
        qr = (rotate_heads(qf, cosine, sine) * HEAD_SIZE**-0.5).astype(jnp.bfloat16)
        zeros = jnp.zeros((pair, HEAD_SIZE), jnp.bfloat16)
        for h in range(qheads):
            q[h, span, :] = jnp.concatenate(
                [qr[:, h * HEAD_SIZE : (h + 1) * HEAD_SIZE], zeros], axis=1
            )
        return 0

    lax.fori_loop(0, chips, project, 0)

    def arrive(chip, _):
        for d in range(1, grp):
            recv_kv(chip, d).wait_recv()
        return 0

    lax.fori_loop(0, chips, arrive, 0)

    key_count = kvb.shape[0]
    chunk = min(key_count, 2048)
    chunks = key_count // chunk
    block = min(256, group_rows)
    tiles = block // rows

    def attention(b, _):
        span = pl.ds(pl.multiple_of(b * block, block), block)
        places = qpos[span, :]
        outs = []
        for h in range(qheads):
            qh = q[h, span, :]

            def visit(t, state):
                top, total, mix = state
                kspan = pl.ds(pl.multiple_of(t * chunk, chunk), chunk)
                kv = kvb[kspan, :]
                scores = lax.dot_general(
                    qh, kv, (((1,), (1,)), ((), ())), preferred_element_type=jnp.float32
                )
                allowed = kpos[:, kspan] <= places
                scores = jnp.where(allowed, scores, neg_large)
                higher = jnp.maximum(top, jnp.max(scores, axis=1, keepdims=True))
                weights = jnp.exp(scores - higher)
                factor = jnp.exp(top - higher)
                total = total * factor + jnp.sum(weights, axis=1, keepdims=True)
                mix = mix * factor + jnp.dot(
                    weights.astype(jnp.bfloat16), kv, preferred_element_type=jnp.float32
                )
                return higher, total, mix

            state = (
                jnp.full((block, 1), sink[s * qheads + h], jnp.float32),
                jnp.ones((block, 1), jnp.float32),
                jnp.zeros((block, LANES), jnp.float32),
            )
            if chunks == 1:
                state = visit(0, state)
            else:
                state = lax.fori_loop(0, chunks, visit, state)
            outs.append((state[2] / state[1])[:, HEAD_SIZE:])
        att = outs[0] if qheads == 1 else jnp.concatenate(outs, axis=1)
        abuf[pl.ds(b * tiles, tiles)] = att.astype(jnp.bfloat16).reshape(tiles, rows, qc)

        def ship(i, _):
            to = b * tiles + i

            @pl.when(to != s)
            def _():
                send_out(to).start()

            return 0

        lax.fori_loop(0, tiles, ship, 0)
        return 0

    lax.fori_loop(0, group_rows // block, attention, 0)
    obuf[s] = abuf[s]

    def drain(j, _):
        @pl.when(j != s)
        def _():
            recv_out(j).wait_recv()
            send_out(j).wait_send()

        return 0

    lax.fori_loop(0, sp, drain, 0)
    for j in range(sp):
        out[:, j * qc : (j + 1) * qc] = obuf[j]
    send_tok(partner).wait_send()

    def finish(k, _):
        send_tok((c + k) % chips * 2 + par).wait_send()
        forward((c + chips - k) % chips * 2 + par).wait_send()
        return 0

    lax.fori_loop(1, chips, finish, 0)

    def finish_kv(chip, _):
        for d in range(1, grp):
            send_kv(chip, d).wait_send()
        return 0

    lax.fori_loop(0, chips, finish_kv, 0)


def per_device(tokens, query_weight, key_value_weight, block_places, sinks):
    sp = lax.axis_size("sp")
    grp = lax.axis_size("grp")
    rows, width = tokens.shape
    group_rows = rows * sp
    key_count = grp * group_rows
    qc = query_weight.shape[1]
    qheads = qc // HEAD_SIZE
    kv_total = key_value_weight.shape[1] // (2 * HEAD_SIZE)
    freq = jnp.arange(HEAD_SIZE // 2, dtype=jnp.float32)
    inverse = rope_base ** (-(freq * 2.0) / HEAD_SIZE)
    inverse = jnp.tile(inverse, LANES // (HEAD_SIZE // 2)).reshape(1, LANES)

    vmem = pl.BlockSpec(memory_space=pltpu.VMEM)
    hbm = pl.BlockSpec(memory_space=pl.ANY)
    smem = pl.BlockSpec(memory_space=pltpu.SMEM)
    dma = pltpu.SemaphoreType.DMA
    return pl.pallas_call(
        functools.partial(kernel, grp, sp, qheads, kv_total),
        out_shape=jax.ShapeDtypeStruct((rows, qc * sp), jnp.bfloat16),
        in_specs=[vmem, hbm, hbm, vmem, smem, smem],
        out_specs=vmem,
        scratch_shapes=[
            pltpu.VMEM((sp, rows, width), jnp.bfloat16),
            pltpu.VMEM((width, qc), jnp.bfloat16),
            pltpu.VMEM((width, 2 * LANES), jnp.bfloat16),
            pltpu.VMEM((key_count, LANES), jnp.bfloat16),
            pltpu.VMEM((qheads, group_rows, LANES), jnp.bfloat16),
            pltpu.VMEM((sp, rows, qc), jnp.bfloat16),
            pltpu.VMEM((sp, rows, qc), jnp.bfloat16),
            pltpu.VMEM((group_rows, LANES), jnp.float32),
            pltpu.VMEM((group_rows, LANES), jnp.float32),
            pltpu.VMEM((group_rows, 1), jnp.int32),
            pltpu.VMEM((1, key_count), jnp.int32),
            dma((3,)),
            dma((sp,)),
            dma((sp,)),
            dma((sp,)),
            dma((grp, sp // 2)),
            dma((grp, sp // 2)),
            dma((sp,)),
            dma((sp,)),
        ],
        compiler_params=pltpu.CompilerParams(
            has_side_effects=True, vmem_limit_bytes=60 * 1024 * 1024
        ),
    )(tokens, query_weight, key_value_weight, inverse, block_places, sinks)


def solution(mesh):
    in_specs = (P(("grp", "sp"), None), P(None, "sp"), P(), P(), P())
    out_specs = P(("grp", "sp"), None)
    return jax.shard_map(
        per_device, mesh=mesh, in_specs=in_specs, out_specs=out_specs, check_vma=False
    )
```

profile of v0, /device:TPU:0, one launch (start us, length us, event | category | flops | bytes accessed | tf_op | source)
XLA Modules:
  0.0 51.6 jit_solution(9789056555557980942)
XLA Ops:
  0.0 0.6 %reshape_tile.3.inverse_ref = f32[1,128]{1,0:T(1,128)} reshape(f32[4,32]{1,0:T(4,128)S(1)} %tile.2) | data formatting | bytes 1024 | tf_op jit(solution)/shard_map/reshape;tile | solution.py:276
  0.6 49.3 %shard_map.55 = bf16[64,2048]{1,0:T(8,128)(2,1)} custom-call(bf16[64,2880]{1,0:T(8,128)(2,1)} %tok.1, bf16[2880,256]{1,0:T(8,128)(2,1)} %wq_any.1, bf16[2880,1024]{1,0:T(8,128)(2,1)} %kvw_any.1, f32[1,128]{1,0:T(1,128)} %reshape_tile.3.inverse_ref, s32[16]{0:T(128)} %places_ref.1, f32[32]{0:T(128)} %sink.1), custom_call_target="tpu_custom_call" | custom-call | tf_op jit(solution)/shard_map/pallas_call | solution.py:282
  49.9 1.7 %copy.7 = bf16[64,2048]{1,0:T(8,128)(2,1)} copy(bf16[64,2048]{1,0:T(8,128)(2,1)} %shard_map.55) | data formatting | bytes 524288
  (2 shorter events, 0.0 us)
where the time goes:
time: 51.8 us; the launch traced here: 51.6 us
  Pallas kernels  49.3 us (95%)
  local copies, waits for them, and re-layouts  2.28 us (4%)
    pallas_call x1, Pallas kernels, per_device(): pl.pallas_call(functools.partial(kernel, grp, sp, qheads, kv_total), out_...  49.3 us
    unnamed x1, local copies, waits for them, and re-layouts  1.67 us

commit v1 on v0

--- a/solution.py
+++ b/solution.py
@@ -311,9 +311,496 @@
     )(tokens, query_weight, key_value_weight, inverse, block_places, sinks)
 
 
+def plane_kernel(
+    grp, sp, qheads,
+    tok_any, wq_any, kvw_any, places, sinks, out,
+    toks, wq, kvw, kvo, kvb, kaug, vt, qs, sbuf, pbuf, abuf, obuf, cos_ref, sin_ref, kpos,
+    wsem, xsend, ysend, psend, rsend, fsend, trecv, ksend, krecv, zsend, zrecv, osend, orecv,
+):
+    s = lax.axis_index("sp")
+    g = lax.axis_index("grp")
+    rows, width = toks.shape[1:]
+    pieces = xsend.shape[0]
+    piece_rows = rows // pieces
+    half = pieces // 2
+    pair = 2 * rows
+    group_rows = rows * sp
+    chips = sp // 2
+    qc = qheads * HEAD_SIZE
+    blocks = grp * BPG
+    dim = HEAD_SIZE // 2
+    p = s % 2
+    c = s // 2
+    cx = c + 1 - 2 * (c % 2)
+    cy = (c + chips // 2) % chips
+    cd = (cx + chips // 2) % chips
+    xn, yn, dn, pn = cx * 2 + p, cy * 2 + p, cd * 2 + p, c * 2 + 1 - p
+    key_base = g * group_rows
+
+    chip_order = [cx, cy, cd, c]
+    wcopies = []
+    for k, chip in enumerate(chip_order):
+        koff = pl.multiple_of(chip * LANES, LANES)
+        voff = pl.multiple_of(sp * HEAD_SIZE + chip * LANES, LANES)
+        wcopies.append([
+            pltpu.make_async_copy(
+                kvw_any.at[:, pl.ds(off, LANES)],
+                kvw.at[k, :, pl.ds(part * LANES, LANES)],
+                wsem.at[2 + 2 * k + part],
+            )
+            for part, off in enumerate((koff, voff))
+        ])
+    tok_copy = pltpu.make_async_copy(tok_any, toks.at[s], wsem.at[0])
+    wq_copy = pltpu.make_async_copy(wq_any, wq, wsem.at[1])
+    tok_copy.start()
+    for pair_copies in wcopies:
+        for copy in pair_copies:
+            copy.start()
+    wq_copy.start()
+
+    barrier = pltpu.get_barrier_semaphore()
+    for to in (xn, yn, dn, pn, cd * 2 + 1 - p, cx * 2 + 1 - p, cy * 2 + 1 - p):
+        pl.semaphore_signal(barrier, inc=1, device_id={"sp": to})
+
+    @pl.when(g > 0)
+    def _():
+        pl.semaphore_signal(barrier, inc=1, device_id={"grp": g - 1})
+
+    @pl.when(g < grp - 1)
+    def _():
+        pl.semaphore_signal(barrier, inc=1, device_id={"grp": g + 1})
+
+    def send_piece(slot, q, to, sem):
+        span = pl.ds(q * piece_rows, piece_rows)
+        return pltpu.make_async_remote_copy(
+            src_ref=toks.at[slot, span], dst_ref=toks.at[slot, span], send_sem=sem,
+            recv_sem=trecv.at[slot, q], device_id={"sp": to},
+        )
+
+    def send_own(slot, to):
+        return pltpu.make_async_remote_copy(
+            src_ref=toks.at[slot], dst_ref=toks.at[slot], send_sem=psend.at[0],
+            recv_sem=trecv.at[slot, 0], device_id={"sp": to},
+        )
+
+    def send_x(q):
+        return send_piece(s, q, xn, xsend.at[q])
+
+    def send_y(q):
+        return send_piece(s, q, yn, ysend.at[q])
+
+    def relay(q):
+        if q >= half:
+            return send_piece(xn, q, yn, rsend.at[q])
+        return send_piece(yn, q, xn, rsend.at[q])
+
+    def forward(k, q):
+        return send_piece((xn, yn, dn)[k], q, pn, fsend.at[k, q])
+
+    def send_head(i, to):
+        span = pl.ds(pl.multiple_of(key_base + s * rows, rows), rows)
+        return pltpu.make_async_remote_copy(
+            src_ref=kvo.at[i], dst_ref=kvb.at[span], send_sem=ksend.at[i],
+            recv_sem=krecv.at[s], device_id={"sp": to},
+        )
+
+    def recv_head(src):
+        span = pl.ds(pl.multiple_of(key_base + src * rows, rows), rows)
+        pltpu.make_async_remote_copy(
+            src_ref=kvo.at[0], dst_ref=kvb.at[span], send_sem=ksend.at[0],
+            recv_sem=krecv.at[src], device_id={"sp": src},
+        ).wait_recv()
+
+    def send_chunk(group, chip, to, way):
+        span = pl.ds(pl.multiple_of(group * group_rows + chip * pair, pair), pair)
+        return pltpu.make_async_remote_copy(
+            src_ref=kvb.at[span], dst_ref=kvb.at[span], send_sem=zsend.at[way, chip],
+            recv_sem=zrecv.at[group, chip], device_id={"grp": to},
+        )
+
+    def share(chip):
+        @pl.when(g > 0)
+        def _():
+            send_chunk(g, chip, g - 1, 0).start()
+
+        @pl.when(g < grp - 1)
+        def _():
+            send_chunk(g, chip, g + 1, 1).start()
+
+    inner = jnp.logical_and(g > 0, g < grp - 1)
+    others = [g + 1 - 2 * (g % 2), 2 - g // 2, 3 - 3 * (g // 2)]
+    targets = [3 - g, 3 * (g // 2), 3 * (g // 2)]
+
+    def recv_group(k):
+        for chip in range(chips):
+            send_chunk(others[k], chip, targets[k], 2 + k).wait_recv()
+
+            @pl.when(inner)
+            def _():
+                send_chunk(others[k], chip, targets[k], 2 + k).start()
+
+    wide = lax.broadcasted_iota(jnp.int32, (1, LANES), 1)
+    inverse = jnp.ones((1, LANES), jnp.float32)
+    bit = 1
+    while bit < dim:
+        factor = rope_base ** (-2.0 * bit / HEAD_SIZE)
+        inverse = jnp.where(wide // bit % 2 == 1, inverse * factor, inverse)
+        bit *= 2
+    sign = jnp.where(wide % HEAD_SIZE < dim, -1.0, 1.0)
+    for j in range(BPG):
+        rspan = slice(j * pair, (j + 1) * pair)
+        within = lax.broadcasted_iota(jnp.int32, (pair, LANES), 0)
+        place = places[g * BPG + j] * pair + within
+        kpos[rspan, :] = place
+        angles = place.astype(jnp.float32) * inverse
+        cos_ref[rspan, :] = jnp.cos(angles)
+        sin_ref[rspan, :] = jnp.sin(angles) * sign
+    block_place = jnp.full((1, LANES), -1, jnp.int32)
+    for e in range(blocks):
+        block_place = jnp.where(wide == HEAD_SIZE + e, places[e], block_place)
+
+    tok_copy.wait()
+    pl.semaphore_wait(barrier, 7 + jnp.minimum(g, 1) + jnp.minimum(grp - 1 - g, 1))
+    send_own(s, pn).start()
+    send_x(half).start()
+    send_y(0).start()
+
+    own_x = toks[s]
+    own_span = pl.ds(pl.multiple_of(s * rows, rows), rows)
+    own_cos, own_sin = cos_ref[own_span, :], sin_ref[own_span, :]
+    low = lax.broadcasted_iota(jnp.int32, (rows, LANES), 1) < HEAD_SIZE
+    for k, chip in enumerate(chip_order):
+        for copy in wcopies[k]:
+            copy.wait()
+        kv = jnp.dot(own_x, kvw[k], preferred_element_type=jnp.float32)
+        keys = rotate_heads(kv[:, :LANES], own_cos, own_sin)
+        values = kv[:, LANES:]
+        first = jnp.where(low, keys, pltpu.roll(values, HEAD_SIZE, 1)).astype(jnp.bfloat16)
+        second = jnp.where(low, pltpu.roll(keys, HEAD_SIZE, 1), values).astype(jnp.bfloat16)
+        if k < chips - 1:
+            kvo[2 * k] = first
+            kvo[2 * k + 1] = second
+            send_head(2 * k, chip * 2).start()
+            send_head(2 * k + 1, chip * 2 + 1).start()
+        else:
+            mine = p == 0
+            kvb[pl.ds(pl.multiple_of(key_base + s * rows, rows), rows), :] = jnp.where(mine, first, second)
+            kvo[2 * k] = jnp.where(mine, second, first)
+            send_head(2 * k, pn).start()
+
+    for q in range(1, half):
+        send_x(half + q).start()
+        send_y(q).start()
+    for q in range(half):
+        send_x(q).start()
+        send_y(half + q).start()
+
+    quarter = rows // 2
+    units = [
+        [(c, 0, 0), (c, 0, quarter), (c, 1, 0), (c, 1, quarter)],
+        [(cx, 0, quarter), (cx, 1, quarter), (cy, 0, 0), (cy, 1, 0)],
+        [(cx, 0, 0), (cx, 1, 0), (cy, 0, quarter), (cy, 1, quarter)],
+        [(cd, 0, 0), (cd, 0, quarter), (cd, 1, 0), (cd, 1, quarter)],
+    ]
+
+    def seg_rows(ref, seg):
+        chip, core, off = seg
+        return ref[pl.ds(pl.multiple_of(chip * pair + core * rows + off, quarter), quarter), :]
+
+    def project(u):
+        segs = units[u]
+        x = jnp.concatenate([toks[chip * 2 + core, off : off + quarter] for chip, core, off in segs], axis=0)
+        cosine = jnp.concatenate([seg_rows(cos_ref, seg) for seg in segs], axis=0)
+        sine = jnp.concatenate([seg_rows(sin_ref, seg) for seg in segs], axis=0)
+        qf = jnp.dot(x, wq[...], preferred_element_type=jnp.float32)
+        qr = rotate_heads(qf, cosine, sine) * HEAD_SIZE**-0.5
+        hidden = jnp.concatenate([
+            jnp.broadcast_to(
+                jnp.where(block_place > places[g * BPG + chip], neg_large, 0.0), (quarter, LANES)
+            )
+            for chip, _, _ in segs
+        ], axis=0)
+        lower = lax.broadcasted_iota(jnp.int32, (pair, LANES), 1) < HEAD_SIZE
+        for h in range(qheads):
+            v = qr[:, h // 2 * LANES : (h // 2 + 1) * LANES]
+            if h % 2:
+                v = pltpu.roll(v, HEAD_SIZE, 1)
+            qs[u, h * pair : (h + 1) * pair, :] = jnp.where(lower, v, hidden).astype(jnp.bfloat16)
+
+    def query_places(u):
+        lane = lax.broadcasted_iota(jnp.int32, (1, pair), 1)
+        place = jnp.zeros((1, pair), jnp.int32)
+        for i, (chip, core, off) in enumerate(units[u]):
+            base = places[g * BPG + chip] * pair + core * rows + off
+            place = jnp.where(lane // quarter == i, base + lane % quarter, place)
+        return place
+
+    def prepare(k):
+        group = g if k == 0 else others[k - 1]
+        lane = lax.broadcasted_iota(jnp.int32, (pair, LANES), 1)
+        for j in range(chips):
+            kv = kvb[pl.ds(pl.multiple_of(group * group_rows + j * pair, pair), pair), :]
+            mark = jnp.where(lane == HEAD_SIZE + group * BPG + j, 1.0, 0.0).astype(jnp.bfloat16)
+            span = slice(k * group_rows + j * pair, k * group_rows + (j + 1) * pair)
+            kaug[span, :] = jnp.where(lane < HEAD_SIZE, kv, mark)
+            vt[:, span] = jnp.transpose(kv)[HEAD_SIZE:]
+
+    sink_row = jnp.concatenate(
+        [jnp.full((1, pair), sinks[s * qheads + h], jnp.float32) for h in range(qheads)], axis=1
+    )
+    tops = [sink_row for _ in units]
+
+    def score(u, k):
+        for j in range(0, chips, 2):
+            span = slice(k * group_rows + j * pair, k * group_rows + (j + 2) * pair)
+            part = lax.dot_general(
+                kaug[span, :], qs[u], (((1,), (1,)), ((), ())), preferred_element_type=jnp.float32
+            )
+            if k == 0:
+                seen = kpos[j * pair : (j + 2) * pair, :] <= query_places(u)
+                part = jnp.where(jnp.concatenate([seen] * qheads, axis=1), part, neg_large)
+            sbuf[u, span, :] = part
+            tops[u] = jnp.maximum(tops[u], jnp.max(part, axis=0, keepdims=True))
+
+    def send_out(u, i):
+        chip, core, off = units[u][i]
+        count = rows if u in (0, 3) else quarter
+        src = abuf.at[u, pl.ds(i * quarter, count)]
+        dst = obuf.at[pl.ds(off, count), pl.ds(pl.multiple_of(s * qc, qc), qc)]
+        return pltpu.make_async_remote_copy(
+            src_ref=src, dst_ref=dst, send_sem=osend.at[u, i],
+            recv_sem=orecv.at[s, u // 2], device_id={"sp": chip * 2 + core},
+        )
+
+    def send_out_partner():
+        src = abuf.at[0, pl.ds(pl.multiple_of((1 - p) * rows, rows), rows)]
+        dst = obuf.at[:, pl.ds(pl.multiple_of(s * qc, qc), qc)]
+        return pltpu.make_async_remote_copy(
+            src_ref=src, dst_ref=dst, send_sem=osend.at[0, 0],
+            recv_sem=orecv.at[s, 0], device_id={"sp": pn},
+        )
+
+    def recv_out(src, off, count, part):
+        dst = obuf.at[pl.ds(off, count), pl.ds(pl.multiple_of(src * qc, qc), qc)]
+        pltpu.make_async_remote_copy(
+            src_ref=abuf.at[0, pl.ds(0, count)], dst_ref=dst, send_sem=osend.at[0, 0],
+            recv_sem=orecv.at[src, part], device_id={"sp": src},
+        ).wait_recv()
+
+    def attend(u):
+        top = tops[u]
+        total = jnp.exp(sink_row - top)
+        keys = sbuf.shape[1]
+        step = 2 * pair
+        for j in range(0, keys, step):
+            weights = jnp.exp(sbuf[u, j : j + step, :] - top)
+            pbuf[j : j + step, :] = weights.astype(jnp.bfloat16)
+            total = total + jnp.sum(weights, axis=0, keepdims=True)
+        mix = jnp.dot(vt[...], pbuf[...], preferred_element_type=jnp.float32) / total
+        heads = [jnp.transpose(mix[:, h * pair : (h + 1) * pair]) for h in range(qheads)]
+        abuf[u] = jnp.concatenate(heads, axis=1).astype(jnp.bfloat16)
+
+    def ship(u):
+        if u == 0:
+            send_out_partner().start()
+            obuf[:, pl.ds(pl.multiple_of(s * qc, qc), qc)] = abuf[
+                0, pl.ds(pl.multiple_of(p * rows, rows), rows), :
+            ]
+        elif u == 3:
+            send_out(u, 0).start()
+            send_out(u, 2).start()
+        else:
+            for i in range(4):
+                send_out(u, i).start()
+
+    def stage(k):
+        qx, qy = (k + half) % pieces, k
+        forward(0, qx).wait_recv()
+        if k < half:
+            relay(qx).start()
+        forward(0, qx).start()
+        forward(1, qy).wait_recv()
+        if k < half:
+            relay(qy).start()
+        forward(1, qy).start()
+
+    def stage_partner(k):
+        qx, qy = (k + half) % pieces, k
+        send_piece(cx * 2 + 1 - p, qx, pn, fsend.at[0, qx]).wait_recv()
+        send_piece(cy * 2 + 1 - p, qy, pn, fsend.at[1, qy]).wait_recv()
+
+    def stage_far(q):
+        for r in (q, q + half):
+            forward(2, r).wait_recv()
+            forward(2, r).start()
+
+    def stage_far_partner(q):
+        for r in (q, q + half):
+            send_piece(cd * 2 + 1 - p, r, pn, fsend.at[2, r]).wait_recv()
+
+    send_own(pn, pn).wait_recv()
+    wq_copy.wait()
+    project(0)
+    recv_head(pn)
+    share(c)
+    stage(0)
+    for chip in (cx, cy, cd):
+        recv_head(chip * 2)
+        recv_head(chip * 2 + 1)
+        share(chip)
+    prepare(0)
+    score(0, 0)
+    stage(1)
+    recv_group(0)
+    prepare(1)
+    score(0, 1)
+    for k in range(half):
+        stage_partner(k)
+    project(1)
+    score(1, 0)
+    score(1, 1)
+    stage(2)
+    recv_group(1)
+    prepare(2)
+    score(0, 2)
+    score(1, 2)
+    stage(3)
+    for k in range(half, pieces):
+        stage_partner(k)
+    project(2)
+    score(2, 0)
+    score(2, 1)
+    score(2, 2)
+    recv_group(2)
+    prepare(3)
+    score(0, 3)
+    score(1, 3)
+    score(2, 3)
+    stage_far(0)
+    attend(0)
+    ship(0)
+    attend(1)
+    ship(1)
+    stage_far(1)
+    attend(2)
+    ship(2)
+    for q in range(half):
+        stage_far_partner(q)
+    project(3)
+    for k in range(grp):
+        score(3, k)
+    attend(3)
+    ship(3)
+
+    recv_out(pn, 0, rows, 0)
+    for core in range(2):
+        recv_out(cx * 2 + core, quarter, quarter, 0)
+        recv_out(cy * 2 + core, 0, quarter, 0)
+        recv_out(cx * 2 + core, 0, quarter, 1)
+        recv_out(cy * 2 + core, quarter, quarter, 1)
+        recv_out(cd * 2 + core, 0, rows, 1)
+    out[...] = obuf[...]
+    send_own(s, pn).wait_send()
+    for q in range(pieces):
+        send_x(q).wait_send()
+        send_y(q).wait_send()
+        relay(q).wait_send()
+        for k in range(3):
+            forward(k, q).wait_send()
+    for i in range(sp - 1):
+        send_head(i, pn).wait_send()
+    for chip in range(chips):
+
+        @pl.when(g > 0)
+        def _():
+            send_chunk(g, chip, g - 1, 0).wait_send()
+
+        @pl.when(g < grp - 1)
+        def _():
+            send_chunk(g, chip, g + 1, 1).wait_send()
+
+        @pl.when(inner)
+        def _():
+            for k in range(3):
+                send_chunk(others[k], chip, targets[k], 2 + k).wait_send()
+
+    send_out_partner().wait_send()
+    for i in range(4):
+        send_out(1, i).wait_send()
+        send_out(2, i).wait_send()
+    send_out(3, 0).wait_send()
+    send_out(3, 2).wait_send()
+
+
+def per_plane(tokens, query_weight, key_value_weight, block_places, sinks):
+    sp = lax.axis_size("sp")
+    grp = lax.axis_size("grp")
+    rows, width = tokens.shape
+    group_rows = rows * sp
+    key_count = grp * group_rows
+    qc = query_weight.shape[1]
+    qheads = qc // HEAD_SIZE
+    pair = 2 * rows
+    columns = qheads * pair
+    pieces = 4
+    hbm = pl.BlockSpec(memory_space=pl.ANY)
+    smem = pl.BlockSpec(memory_space=pltpu.SMEM)
+    dma = pltpu.SemaphoreType.DMA
+    bf16, f32 = jnp.bfloat16, jnp.float32
+    return pl.pallas_call(
+        functools.partial(plane_kernel, grp, sp, qheads),
+        out_shape=jax.ShapeDtypeStruct((rows, qc * sp), bf16),
+        in_specs=[hbm, hbm, hbm, smem, smem],
+        out_specs=pl.BlockSpec(memory_space=pltpu.VMEM),
+        scratch_shapes=[
+            pltpu.VMEM((sp, rows, width), bf16),
+            pltpu.VMEM((width, qc), bf16),
+            pltpu.VMEM((sp // 2, width, 2 * LANES), bf16),
+            pltpu.VMEM((sp, rows, LANES), bf16),
+            pltpu.VMEM((key_count, LANES), bf16),
+            pltpu.VMEM((key_count, LANES), bf16),
+            pltpu.VMEM((HEAD_SIZE, key_count), bf16),
+            pltpu.VMEM((sp // 2, columns, LANES), bf16),
+            pltpu.VMEM((sp // 2, key_count, columns), f32),
+            pltpu.VMEM((key_count, columns), bf16),
+            pltpu.VMEM((sp // 2, pair, qc), bf16),
+            pltpu.VMEM((rows, qc * sp), bf16),
+            pltpu.VMEM((group_rows, LANES), f32),
+            pltpu.VMEM((group_rows, LANES), f32),
+            pltpu.VMEM((group_rows, LANES), jnp.int32),
+            dma((2 + sp,)),
+            dma((pieces,)),
+            dma((pieces,)),
+            dma((1,)),
+            dma((pieces,)),
+            dma((3, pieces)),
+            dma((sp, pieces)),
+            dma((sp,)),
+            dma((sp,)),
+            dma((5, sp // 2)),
+            dma((grp, sp // 2)),
+            dma((4, 4)),
+            dma((sp, 2)),
+        ],
+        compiler_params=pltpu.CompilerParams(
+            has_side_effects=True, collective_id=0, vmem_limit_bytes=60 * 1024 * 1024
+        ),
+    )(tokens, query_weight, key_value_weight, block_places, sinks)
+
+
+def local_form(tokens, query_weight, key_value_weight, block_places, sinks):
+    sp = lax.axis_size("sp")
+    grp = lax.axis_size("grp")
+    heads = query_weight.shape[1] // HEAD_SIZE
+    kv_total = key_value_weight.shape[1] // (2 * HEAD_SIZE)
+    square = sp // 2 == BPG and grp == BPG and kv_total == sp and block_places.shape[0] == grp * BPG
+    form = per_plane if square and heads * HEAD_SIZE == 2 * LANES else per_device
+    return form(tokens, query_weight, key_value_weight, block_places, sinks)
+
+
 def solution(mesh):
     in_specs = (P(("grp", "sp"), None), P(None, "sp"), P(), P(), P())
     out_specs = P(("grp", "sp"), None)
     return jax.shard_map(
-        per_device, mesh=mesh, in_specs=in_specs, out_specs=out_specs, check_vma=False
+        local_form, mesh=mesh, in_specs=in_specs, out_specs=out_specs, check_vma=False
     )

time: 51.8 us -> 37.2 us (0.72)
  Pallas kernels: 49.3 us -> 35.3 us
  local copies, waits for them, and re-layouts: 2.28 us -> 1.67 us
    pallas_call x1, Pallas kernels: 49.3 us -> 35.3 us  [per_plane(): pl.pallas_call(functools.partial(plane_kernel, grp, sp, qheads), out_shap...]
    another operation x2 -> x0, local copies, waits for them, and re-layouts: 0.61 us -> none  [per_device(): inverse = jnp.tile(inverse, LANES // (HEAD_SIZE // 2)).reshape(1, LANES)]
where the time goes in v1:
time: 37.2 us; the launch traced here: 37 us
  Pallas kernels  35.3 us (95%)
  local copies, waits for them, and re-layouts  1.67 us (4%)
    pallas_call x1, Pallas kernels, per_plane(): pl.pallas_call(functools.partial(plane_kernel, grp, sp, qheads), out_shap...  35.3 us
    unnamed x1, local copies, waits for them, and re-layouts  1.67 us

profile of v1, /device:TPU:0, one launch (start us, length us, event | category | flops | bytes accessed | tf_op | source)
XLA Modules:
  0.0 37.0 jit_solution(6275691398435977975)
XLA Ops:
  0.0 35.3 %shard_map.55 = bf16[64,2048]{1,0:T(8,128)(2,1)} custom-call(bf16[64,2880]{1,0:T(8,128)(2,1)} %tok_any.1, bf16[2880,256]{1,0:T(8,128)(2,1)} %wq_any.1, bf16[2880,1024]{1,0:T(8,128)(2,1)} %kvw_any.1, s32[16]{0:T(128)} %places.1, f32[32]{0:T(128)} %sinks.1), custom_call_target="tpu_custom_call" | custom-call | tf_op jit(solution)/shard_map/pallas_call | solution.py:750
  35.3 1.7 %copy.7 = bf16[64,2048]{1,0:T(8,128)(2,1)} copy(bf16[64,2048]{1,0:T(8,128)(2,1)} %shard_map.55) | data formatting | bytes 524288

commit v2 on v1

--- a/solution.py
+++ b/solution.py
@@ -313,8 +313,8 @@
 
 def plane_kernel(
     grp, sp, qheads,
-    tok_any, wq_any, kvw_any, places, sinks, out,
-    toks, wq, kvw, kvo, kvb, kaug, vt, qs, sbuf, pbuf, abuf, obuf, cos_ref, sin_ref, kpos,
+    tok_any, wq_any, kvw_any, places_any, sinks_any, out,
+    places, sinks,    toks, wq, kvw, kvo, kvb, kaug, vt, qs, sbuf, pbuf, mbuf, abuf, obuf, cos_ref, sin_ref, kpos,
     wsem, xsend, ysend, psend, rsend, fsend, trecv, ksend, krecv, zsend, zrecv, osend, orecv,
 ):
     s = lax.axis_index("sp")
@@ -337,7 +337,7 @@
     xn, yn, dn, pn = cx * 2 + p, cy * 2 + p, cd * 2 + p, c * 2 + 1 - p
     key_base = g * group_rows
 
-    chip_order = [cx, cy, cd, c]
+    chip_order = [c, cd, cx, cy]
     wcopies = []
     for k, chip in enumerate(chip_order):
         koff = pl.multiple_of(chip * LANES, LANES)
@@ -345,13 +345,17 @@
         wcopies.append([
             pltpu.make_async_copy(
                 kvw_any.at[:, pl.ds(off, LANES)],
-                kvw.at[k, :, pl.ds(part * LANES, LANES)],
+                kvw.at[k // 2, :, pl.ds((2 * (k % 2) + part) * LANES, LANES)],
                 wsem.at[2 + 2 * k + part],
             )
             for part, off in enumerate((koff, voff))
         ])
     tok_copy = pltpu.make_async_copy(tok_any, toks.at[s], wsem.at[0])
     wq_copy = pltpu.make_async_copy(wq_any, wq, wsem.at[1])
+    pcopy = pltpu.make_async_copy(places_any, places, wsem.at[2 + sp])
+    scopy = pltpu.make_async_copy(sinks_any, sinks, wsem.at[3 + sp])
+    pcopy.start()
+    scopy.start()
     tok_copy.start()
     for pair_copies in wcopies:
         for copy in pair_copies:
@@ -421,24 +425,29 @@
     def share(chip):
         @pl.when(g > 0)
         def _():
-            send_chunk(g, chip, g - 1, 0).start()
+            send_chunk(g, chip, g - 1, 1).start()
 
         @pl.when(g < grp - 1)
         def _():
-            send_chunk(g, chip, g + 1, 1).start()
+            send_chunk(g, chip, g + 1, 0).start()
 
     inner = jnp.logical_and(g > 0, g < grp - 1)
-    others = [g + 1 - 2 * (g % 2), 2 - g // 2, 3 - 3 * (g // 2)]
-    targets = [3 - g, 3 * (g // 2), 3 * (g // 2)]
+    others = [jnp.abs(g - 1), 2 + g // 2 - 2 * (g // 3), 3 - 3 * (g // 2)]
+    targets = [g + 1, g - 1, 3 * (g // 2)]
+
+    def pass_on(k, chip):
+        return send_chunk(others[k], chip, targets[k], 2 + k)
 
     def recv_group(k):
         for chip in range(chips):
-            send_chunk(others[k], chip, targets[k], 2 + k).wait_recv()
+            send_chunk(others[k], chip, g, 0).wait_recv()
 
             @pl.when(inner)
             def _():
-                send_chunk(others[k], chip, targets[k], 2 + k).start()
-
+                pass_on(k, chip).start()
+
+    pcopy.wait()
+    scopy.wait()
     wide = lax.broadcasted_iota(jnp.int32, (1, LANES), 1)
     inverse = jnp.ones((1, LANES), jnp.float32)
     bit = 1
@@ -447,6 +456,48 @@
         inverse = jnp.where(wide // bit % 2 == 1, inverse * factor, inverse)
         bit *= 2
     sign = jnp.where(wide % HEAD_SIZE < dim, -1.0, 1.0)
+    own_place = places[g * BPG + c] * pair + p * rows + lax.broadcasted_iota(jnp.int32, (rows, LANES), 0)
+    own_angles = own_place.astype(jnp.float32) * inverse
+    own_cos, own_sin = jnp.cos(own_angles), jnp.sin(own_angles) * sign
+    tok_copy.wait()
+    pl.semaphore_wait(barrier, 7 + jnp.minimum(g, 1) + jnp.minimum(grp - 1 - g, 1))
+    send_own(s, pn).start()
+    send_x(half).start()
+    send_y(0).start()
+
+    own_x = toks[s]
+    low = lax.broadcasted_iota(jnp.int32, (rows, LANES), 1) < HEAD_SIZE
+    for k in range(chips):
+        if k % 2 == 0:
+            for copy in wcopies[k] + wcopies[k + 1]:
+                copy.wait()
+            both = jnp.dot(own_x, kvw[k // 2], preferred_element_type=jnp.float32)
+        kv = both[:, k % 2 * 2 * LANES : (k % 2 + 1) * 2 * LANES]
+        keys = rotate_heads(kv[:, :LANES], own_cos, own_sin)
+        values = kv[:, LANES:]
+        first = jnp.where(low, keys, pltpu.roll(values, HEAD_SIZE, 1)).astype(jnp.bfloat16)
+        second = jnp.where(low, pltpu.roll(keys, HEAD_SIZE, 1), values).astype(jnp.bfloat16)
+        if k == 0:
+            mine = p == 0
+            kvb[pl.ds(pl.multiple_of(key_base + s * rows, rows), rows), :] = jnp.where(mine, first, second)
+            kvo[0] = jnp.where(mine, second, first)
+            send_head(0, pn).start()
+        else:
+            chip = chip_order[k]
+            kvo[2 * k - 1] = first
+            kvo[2 * k] = second
+            send_head(2 * k - 1, chip * 2).start()
+            send_head(2 * k, chip * 2 + 1).start()
+
+    for q in range(1, half):
+        send_x(half + q).start()
+        send_y(q).start()
+    for q in range(half):
+        send_x(q).start()
+        send_y(half + q).start()
+
+    recv_head(pn)
+    share(c)
     for j in range(BPG):
         rspan = slice(j * pair, (j + 1) * pair)
         within = lax.broadcasted_iota(jnp.int32, (pair, LANES), 0)
@@ -458,42 +509,6 @@
     block_place = jnp.full((1, LANES), -1, jnp.int32)
     for e in range(blocks):
         block_place = jnp.where(wide == HEAD_SIZE + e, places[e], block_place)
-
-    tok_copy.wait()
-    pl.semaphore_wait(barrier, 7 + jnp.minimum(g, 1) + jnp.minimum(grp - 1 - g, 1))
-    send_own(s, pn).start()
-    send_x(half).start()
-    send_y(0).start()
-
-    own_x = toks[s]
-    own_span = pl.ds(pl.multiple_of(s * rows, rows), rows)
-    own_cos, own_sin = cos_ref[own_span, :], sin_ref[own_span, :]
-    low = lax.broadcasted_iota(jnp.int32, (rows, LANES), 1) < HEAD_SIZE
-    for k, chip in enumerate(chip_order):
-        for copy in wcopies[k]:
-            copy.wait()
-        kv = jnp.dot(own_x, kvw[k], preferred_element_type=jnp.float32)
-        keys = rotate_heads(kv[:, :LANES], own_cos, own_sin)
-        values = kv[:, LANES:]
-        first = jnp.where(low, keys, pltpu.roll(values, HEAD_SIZE, 1)).astype(jnp.bfloat16)
-        second = jnp.where(low, pltpu.roll(keys, HEAD_SIZE, 1), values).astype(jnp.bfloat16)
-        if k < chips - 1:
-            kvo[2 * k] = first
-            kvo[2 * k + 1] = second
-            send_head(2 * k, chip * 2).start()
-            send_head(2 * k + 1, chip * 2 + 1).start()
-        else:
-            mine = p == 0
-            kvb[pl.ds(pl.multiple_of(key_base + s * rows, rows), rows), :] = jnp.where(mine, first, second)
-            kvo[2 * k] = jnp.where(mine, second, first)
-            send_head(2 * k, pn).start()
-
-    for q in range(1, half):
-        send_x(half + q).start()
-        send_y(q).start()
-    for q in range(half):
-        send_x(q).start()
-        send_y(half + q).start()
 
     quarter = rows // 2
     units = [
@@ -550,7 +565,7 @@
     )
     tops = [sink_row for _ in units]
 
-    def score(u, k):
+    def part_scores(u, k):
         for j in range(0, chips, 2):
             span = slice(k * group_rows + j * pair, k * group_rows + (j + 2) * pair)
             part = lax.dot_general(
@@ -559,8 +574,55 @@
             if k == 0:
                 seen = kpos[j * pair : (j + 2) * pair, :] <= query_places(u)
                 part = jnp.where(jnp.concatenate([seen] * qheads, axis=1), part, neg_large)
+            yield span, part
+
+    def score(u, k):
+        for span, part in part_scores(u, k):
             sbuf[u, span, :] = part
             tops[u] = jnp.maximum(tops[u], jnp.max(part, axis=0, keepdims=True))
+
+    bases = [None for _ in units]
+    totals = [None for _ in units]
+
+    def absorb(us, stored, fresh, final=False):
+        low_key = min(stored + fresh) * group_rows
+        high_key = (max(stored + fresh) + 1) * group_rows
+        parts = {u: [piece for k in fresh for piece in part_scores(u, k)] for u in us}
+        factor, mix = {}, {}
+        for u in us:
+            for _, part in parts[u]:
+                tops[u] = jnp.maximum(tops[u], jnp.max(part, axis=0, keepdims=True))
+            if bases[u] is None:
+                total = jnp.exp(sink_row - tops[u])
+            else:
+                factor[u] = jnp.exp(bases[u] - tops[u])
+                total = totals[u] * factor[u]
+            for k in stored:
+                for j in range(0, chips, 2):
+                    span = slice(k * group_rows + j * pair, k * group_rows + (j + 2) * pair)
+                    weights = jnp.exp(sbuf[u, span, :] - tops[u])
+                    pbuf[u, span, :] = weights.astype(jnp.bfloat16)
+                    total = total + jnp.sum(weights, axis=0, keepdims=True)
+            for span, part in parts[u]:
+                weights = jnp.exp(part - tops[u])
+                pbuf[u, span, :] = weights.astype(jnp.bfloat16)
+                total = total + jnp.sum(weights, axis=0, keepdims=True)
+            totals[u], bases[u] = total, tops[u]
+        for u in us:
+            mix[u] = jnp.dot(
+                vt[:, low_key:high_key], pbuf[u, low_key:high_key, :], preferred_element_type=jnp.float32
+            )
+        for u in us:
+            full = mix[u] + mbuf[u] * factor[u] if u in factor else mix[u]
+            if not final:
+                mbuf[u] = full
+                continue
+            full = full / totals[u]
+            heads = [jnp.transpose(full[:, h * pair : (h + 1) * pair]) for h in range(qheads)]
+            abuf[u] = jnp.concatenate(heads, axis=1).astype(jnp.bfloat16)
+        if final:
+            for u in us:
+                ship(u)
 
     def send_out(u, i):
         chip, core, off = units[u][i]
@@ -586,19 +648,6 @@
             src_ref=abuf.at[0, pl.ds(0, count)], dst_ref=dst, send_sem=osend.at[0, 0],
             recv_sem=orecv.at[src, part], device_id={"sp": src},
         ).wait_recv()
-
-    def attend(u):
-        top = tops[u]
-        total = jnp.exp(sink_row - top)
-        keys = sbuf.shape[1]
-        step = 2 * pair
-        for j in range(0, keys, step):
-            weights = jnp.exp(sbuf[u, j : j + step, :] - top)
-            pbuf[j : j + step, :] = weights.astype(jnp.bfloat16)
-            total = total + jnp.sum(weights, axis=0, keepdims=True)
-        mix = jnp.dot(vt[...], pbuf[...], preferred_element_type=jnp.float32) / total
-        heads = [jnp.transpose(mix[:, h * pair : (h + 1) * pair]) for h in range(qheads)]
-        abuf[u] = jnp.concatenate(heads, axis=1).astype(jnp.bfloat16)
 
     def ship(u):
         if u == 0:
@@ -641,8 +690,6 @@
     send_own(pn, pn).wait_recv()
     wq_copy.wait()
     project(0)
-    recv_head(pn)
-    share(c)
     stage(0)
     for chip in (cx, cy, cd):
         recv_head(chip * 2)
@@ -651,46 +698,40 @@
     prepare(0)
     score(0, 0)
     stage(1)
-    recv_group(0)
-    prepare(1)
-    score(0, 1)
     for k in range(half):
         stage_partner(k)
     project(1)
     score(1, 0)
+    recv_group(0)
+    pl.when(inner)(lambda: recv_group(1))
+    prepare(1)
+    score(0, 1)
     score(1, 1)
     stage(2)
-    recv_group(1)
-    prepare(2)
-    score(0, 2)
-    score(1, 2)
+    absorb((0, 1), [0, 1], [])
     stage(3)
     for k in range(half, pieces):
         stage_partner(k)
     project(2)
     score(2, 0)
     score(2, 1)
-    score(2, 2)
-    recv_group(2)
-    prepare(3)
-    score(0, 3)
-    score(1, 3)
-    score(2, 3)
+    pl.when(jnp.logical_not(inner))(lambda: recv_group(1))
+    pl.when(inner)(lambda: recv_group(2))
     stage_far(0)
-    attend(0)
-    ship(0)
-    attend(1)
-    ship(1)
+    prepare(2)
+    absorb((0, 1), [], [2])
     stage_far(1)
-    attend(2)
-    ship(2)
+    absorb((2,), [0, 1], [2])
     for q in range(half):
         stage_far_partner(q)
     project(3)
-    for k in range(grp):
+    for k in range(grp - 1):
         score(3, k)
-    attend(3)
-    ship(3)
+    pl.when(jnp.logical_not(inner))(lambda: recv_group(2))
+    prepare(3)
+    absorb((3,), [0, 1, 2], [3], True)
+    absorb((1, 2), [], [3], True)
+    absorb((0,), [], [3], True)
 
     recv_out(pn, 0, rows, 0)
     for core in range(2):
@@ -710,19 +751,18 @@
     for i in range(sp - 1):
         send_head(i, pn).wait_send()
     for chip in range(chips):
-
         @pl.when(g > 0)
         def _():
-            send_chunk(g, chip, g - 1, 0).wait_send()
+            send_chunk(g, chip, g - 1, 1).wait_send()
 
         @pl.when(g < grp - 1)
         def _():
-            send_chunk(g, chip, g + 1, 1).wait_send()
+            send_chunk(g, chip, g + 1, 0).wait_send()
 
         @pl.when(inner)
         def _():
             for k in range(3):
-                send_chunk(others[k], chip, targets[k], 2 + k).wait_send()
+                pass_on(k, chip).wait_send()
 
     send_out_partner().wait_send()
     for i in range(4):
@@ -744,31 +784,33 @@
     columns = qheads * pair
     pieces = 4
     hbm = pl.BlockSpec(memory_space=pl.ANY)
-    smem = pl.BlockSpec(memory_space=pltpu.SMEM)
     dma = pltpu.SemaphoreType.DMA
     bf16, f32 = jnp.bfloat16, jnp.float32
     return pl.pallas_call(
         functools.partial(plane_kernel, grp, sp, qheads),
-        out_shape=jax.ShapeDtypeStruct((rows, qc * sp), bf16),
-        in_specs=[hbm, hbm, hbm, smem, smem],
+        out_shape=pltpu.VMEM((rows, qc * sp), bf16),
+        in_specs=[hbm] * 5,
         out_specs=pl.BlockSpec(memory_space=pltpu.VMEM),
         scratch_shapes=[
+            pltpu.SMEM(block_places.shape, block_places.dtype),
+            pltpu.SMEM(sinks.shape, sinks.dtype),
             pltpu.VMEM((sp, rows, width), bf16),
             pltpu.VMEM((width, qc), bf16),
-            pltpu.VMEM((sp // 2, width, 2 * LANES), bf16),
+            pltpu.VMEM((2, width, 4 * LANES), bf16),
             pltpu.VMEM((sp, rows, LANES), bf16),
             pltpu.VMEM((key_count, LANES), bf16),
             pltpu.VMEM((key_count, LANES), bf16),
             pltpu.VMEM((HEAD_SIZE, key_count), bf16),
             pltpu.VMEM((sp // 2, columns, LANES), bf16),
             pltpu.VMEM((sp // 2, key_count, columns), f32),
-            pltpu.VMEM((key_count, columns), bf16),
+            pltpu.VMEM((sp // 2, key_count, columns), bf16),
+            pltpu.VMEM((sp // 2, HEAD_SIZE, columns), f32),
             pltpu.VMEM((sp // 2, pair, qc), bf16),
             pltpu.VMEM((rows, qc * sp), bf16),
             pltpu.VMEM((group_rows, LANES), f32),
             pltpu.VMEM((group_rows, LANES), f32),
             pltpu.VMEM((group_rows, LANES), jnp.int32),
-            dma((2 + sp,)),
+            dma((4 + sp,)),
             dma((pieces,)),
             dma((pieces,)),
             dma((1,)),

time: 37.2 us -> 32.5 us (0.87)
  Pallas kernels: 35.3 us -> 31.7 us
  local copies, waits for them, and re-layouts: 1.67 us -> 0.71 us
    pallas_call x1, Pallas kernels: 35.3 us -> 31.7 us  [per_plane(): pl.pallas_call(functools.partial(plane_kernel, grp, sp, qheads), out_shap...]
    unnamed x1, local copies, waits for them, and re-layouts: 1.67 us -> 0.71 us
where the time goes in v2:
time: 32.5 us; the launch traced here: 32.4 us
  Pallas kernels  31.7 us (98%)
  local copies, waits for them, and re-layouts  0.71 us (2%)
    pallas_call x1, Pallas kernels, per_plane(): pl.pallas_call(functools.partial(plane_kernel, grp, sp, qheads), out_shap...  31.7 us
    unnamed x1, local copies, waits for them, and re-layouts  0.71 us

profile of v2, /device:TPU:0, one launch (start us, length us, event | category | flops | bytes accessed | tf_op | source)
XLA Modules:
  0.0 32.4 jit_solution(9140689431003498147)
XLA Ops:
  0.0 31.7 %shard_map.55 = bf16[64,2048]{1,0:T(8,128)(2,1)S(1)} custom-call(bf16[64,2880]{1,0:T(8,128)(2,1)} %tok_any.1, bf16[2880,256]{1,0:T(8,128)(2,1)} %wq_any.1, bf16[2880,1024]{1,0:T(8,128)(2,1)} %kvw_any.1, s32[16]{0:T(128)} %places_any.1, f32[32]{0:T(128)} %sinks_any.1), custom_call_target="tpu_custom_call" | custom-call | tf_op jit(solution)/shard_map/pallas_call | solution.py:789
  31.7 0.7 %copy.7 = bf16[64,2048]{1,0:T(8,128)(2,1)} copy(bf16[64,2048]{1,0:T(8,128)(2,1)S(1)} %shard_map.55) | data formatting | bytes 524288

commit v3 on v2

--- a/solution.py
+++ b/solution.py
@@ -315,12 +315,12 @@
     grp, sp, qheads,
     tok_any, wq_any, kvw_any, places_any, sinks_any, out,
     places, sinks,    toks, wq, kvw, kvo, kvb, kaug, vt, qs, sbuf, pbuf, mbuf, abuf, obuf, cos_ref, sin_ref, kpos,
-    wsem, xsend, ysend, psend, rsend, fsend, trecv, ksend, krecv, zsend, zrecv, osend, orecv,
+    wsem, tsend, trecv, drecv, ksend, krecv, zsend, zrecv, osend, orecv, ready,
 ):
     s = lax.axis_index("sp")
     g = lax.axis_index("grp")
     rows, width = toks.shape[1:]
-    pieces = xsend.shape[0]
+    pieces = trecv.shape[1]
     piece_rows = rows // pieces
     half = pieces // 2
     pair = 2 * rows
@@ -337,38 +337,40 @@
     xn, yn, dn, pn = cx * 2 + p, cy * 2 + p, cd * 2 + p, c * 2 + 1 - p
     key_base = g * group_rows
 
-    chip_order = [c, cd, cx, cy]
+    chip_order = [c, cx, cy, cd]
+    ways = [0, 2, 3, 1]
     wcopies = []
     for k, chip in enumerate(chip_order):
         koff = pl.multiple_of(chip * LANES, LANES)
         voff = pl.multiple_of(sp * HEAD_SIZE + chip * LANES, LANES)
-        wcopies.append([
-            pltpu.make_async_copy(
-                kvw_any.at[:, pl.ds(off, LANES)],
-                kvw.at[k // 2, :, pl.ds((2 * (k % 2) + part) * LANES, LANES)],
-                wsem.at[2 + 2 * k + part],
+        for part, off in enumerate((koff, voff)):
+            wcopies.append(
+                pltpu.make_async_copy(
+                    kvw_any.at[:, pl.ds(off, LANES)],
+                    kvw.at[k // 2, :, pl.ds((2 * (k % 2) + part) * LANES, LANES)],
+                    wsem.at[2 + k // 2],
+                )
             )
-            for part, off in enumerate((koff, voff))
-        ])
     tok_copy = pltpu.make_async_copy(tok_any, toks.at[s], wsem.at[0])
     wq_copy = pltpu.make_async_copy(wq_any, wq, wsem.at[1])
-    pcopy = pltpu.make_async_copy(places_any, places, wsem.at[2 + sp])
-    scopy = pltpu.make_async_copy(sinks_any, sinks, wsem.at[3 + sp])
+    pcopy = pltpu.make_async_copy(places_any, places, wsem.at[4])
+    scopy = pltpu.make_async_copy(sinks_any, sinks, wsem.at[5])
     pcopy.start()
     scopy.start()
     tok_copy.start()
-    for pair_copies in wcopies:
-        for copy in pair_copies:
-            copy.start()
+    for copy in wcopies:
+        copy.start()
     wq_copy.start()
 
     barrier = pltpu.get_barrier_semaphore()
-    for to in (xn, yn, dn, pn, cd * 2 + 1 - p, cx * 2 + 1 - p, cy * 2 + 1 - p):
+    upper = c >= chips // 2
+    for to in (xn, yn, pn, cx * 2 + 1 - p, cy * 2 + 1 - p):
         pl.semaphore_signal(barrier, inc=1, device_id={"sp": to})
 
-    @pl.when(g > 0)
+    @pl.when(jnp.logical_not(upper))
     def _():
-        pl.semaphore_signal(barrier, inc=1, device_id={"grp": g - 1})
+        for core in range(2):
+            pl.semaphore_signal(barrier, inc=1, device_id={"sp": cd * 2 + core})
 
     @pl.when(g < grp - 1)
     def _():
@@ -377,48 +379,57 @@
     def send_piece(slot, q, to, sem):
         span = pl.ds(q * piece_rows, piece_rows)
         return pltpu.make_async_remote_copy(
-            src_ref=toks.at[slot, span], dst_ref=toks.at[slot, span], send_sem=sem,
-            recv_sem=trecv.at[slot, q], device_id={"sp": to},
+            src_ref=toks.at[slot, span], dst_ref=toks.at[slot, span], send_sem=tsend.at[0],
+            recv_sem=sem, device_id={"sp": to},
         )
 
     def send_own(slot, to):
         return pltpu.make_async_remote_copy(
-            src_ref=toks.at[slot], dst_ref=toks.at[slot], send_sem=psend.at[0],
-            recv_sem=trecv.at[slot, 0], device_id={"sp": to},
+            src_ref=toks.at[slot], dst_ref=toks.at[slot], send_sem=tsend.at[0],
+            recv_sem=drecv.at[3], device_id={"sp": to},
         )
 
     def send_x(q):
-        return send_piece(s, q, xn, xsend.at[q])
+        return send_piece(s, q, xn, trecv.at[0, q])
 
     def send_y(q):
-        return send_piece(s, q, yn, ysend.at[q])
+        return send_piece(s, q, yn, trecv.at[1, q])
 
     def relay(q):
         if q >= half:
-            return send_piece(xn, q, yn, rsend.at[q])
-        return send_piece(yn, q, xn, rsend.at[q])
-
-    def forward(k, q):
-        return send_piece((xn, yn, dn)[k], q, pn, fsend.at[k, q])
-
-    def send_head(i, to):
+            return send_piece(xn, q, yn, trecv.at[2, q])
+        return send_piece(yn, q, xn, trecv.at[2, q])
+
+    def arrived(k, q):
+        send_piece((xn, yn, dn)[k], q, pn, trecv.at[k, q]).wait_recv()
+
+    def forward(k, q, i):
+        return send_piece((xn, yn, dn)[k], q, pn, drecv.at[i])
+
+    def wait_rows(sem, slots, count=rows):
+        area = toks.at[pl.ds(0, slots), pl.ds(0, count)]
+        pltpu.make_async_remote_copy(
+            src_ref=area, dst_ref=area, send_sem=sem, recv_sem=sem, device_id={"sp": pn}
+        ).wait_recv()
+
+    def send_head(i, to, way):
         span = pl.ds(pl.multiple_of(key_base + s * rows, rows), rows)
         return pltpu.make_async_remote_copy(
-            src_ref=kvo.at[i], dst_ref=kvb.at[span], send_sem=ksend.at[i],
-            recv_sem=krecv.at[s], device_id={"sp": to},
-        )
-
-    def recv_head(src):
-        span = pl.ds(pl.multiple_of(key_base + src * rows, rows), rows)
+            src_ref=kvo.at[i], dst_ref=kvb.at[span], send_sem=ksend.at[0],
+            recv_sem=krecv.at[way], device_id={"sp": to},
+        )
+
+    def recv_heads(chip, way):
+        span = pl.ds(pl.multiple_of(key_base + chip * pair, pair), rows if way == 0 else pair)
         pltpu.make_async_remote_copy(
-            src_ref=kvo.at[0], dst_ref=kvb.at[span], send_sem=ksend.at[0],
-            recv_sem=krecv.at[src], device_id={"sp": src},
+            src_ref=kvb.at[span], dst_ref=kvb.at[span], send_sem=ksend.at[0],
+            recv_sem=krecv.at[way], device_id={"sp": pn},
         ).wait_recv()
 
     def send_chunk(group, chip, to, way):
         span = pl.ds(pl.multiple_of(group * group_rows + chip * pair, pair), pair)
         return pltpu.make_async_remote_copy(
-            src_ref=kvb.at[span], dst_ref=kvb.at[span], send_sem=zsend.at[way, chip],
+            src_ref=kvb.at[span], dst_ref=kvb.at[span], send_sem=zsend.at[way],
             recv_sem=zrecv.at[group, chip], device_id={"grp": to},
         )
 
@@ -436,10 +447,12 @@
     targets = [g + 1, g - 1, 3 * (g // 2)]
 
     def pass_on(k, chip):
-        return send_chunk(others[k], chip, targets[k], 2 + k)
-
-    def recv_group(k):
-        for chip in range(chips):
+        return send_chunk(others[k], chip, targets[k], 2)
+
+    outer = jnp.logical_not(inner)
+
+    def recv_group(k, chip_list):
+        for chip in chip_list:
             send_chunk(others[k], chip, g, 0).wait_recv()
 
             @pl.when(inner)
@@ -460,34 +473,47 @@
     own_angles = own_place.astype(jnp.float32) * inverse
     own_cos, own_sin = jnp.cos(own_angles), jnp.sin(own_angles) * sign
     tok_copy.wait()
-    pl.semaphore_wait(barrier, 7 + jnp.minimum(g, 1) + jnp.minimum(grp - 1 - g, 1))
+    pl.semaphore_wait(barrier, 5 + jnp.minimum(g, 1) + 2 * (c // (chips // 2)))
     send_own(s, pn).start()
     send_x(half).start()
     send_y(0).start()
+
+    @pl.when(g > 0)
+    def _():
+        pl.semaphore_signal(ready.at[0], inc=1, device_id={"grp": g - 1})
+
+    @pl.when(upper)
+    def _():
+        for core in range(2):
+            pl.semaphore_signal(ready.at[1], inc=1, device_id={"sp": cd * 2 + core})
 
     own_x = toks[s]
     low = lax.broadcasted_iota(jnp.int32, (rows, LANES), 1) < HEAD_SIZE
     for k in range(chips):
         if k % 2 == 0:
-            for copy in wcopies[k] + wcopies[k + 1]:
-                copy.wait()
+            pltpu.make_async_copy(
+                kvw_any.at[:, pl.ds(0, 4 * LANES)], kvw.at[k // 2], wsem.at[2 + k // 2]
+            ).wait()
             both = jnp.dot(own_x, kvw[k // 2], preferred_element_type=jnp.float32)
         kv = both[:, k % 2 * 2 * LANES : (k % 2 + 1) * 2 * LANES]
         keys = rotate_heads(kv[:, :LANES], own_cos, own_sin)
         values = kv[:, LANES:]
         first = jnp.where(low, keys, pltpu.roll(values, HEAD_SIZE, 1)).astype(jnp.bfloat16)
         second = jnp.where(low, pltpu.roll(keys, HEAD_SIZE, 1), values).astype(jnp.bfloat16)
-        if k == 0:
+        way = ways[k]
+        if way == 0:
             mine = p == 0
             kvb[pl.ds(pl.multiple_of(key_base + s * rows, rows), rows), :] = jnp.where(mine, first, second)
             kvo[0] = jnp.where(mine, second, first)
-            send_head(0, pn).start()
+            send_head(0, pn, 0).start()
         else:
             chip = chip_order[k]
-            kvo[2 * k - 1] = first
-            kvo[2 * k] = second
-            send_head(2 * k - 1, chip * 2).start()
-            send_head(2 * k, chip * 2 + 1).start()
+            kvo[2 * way - 1] = first
+            kvo[2 * way] = second
+            if way == 1:
+                pl.when(jnp.logical_not(upper))(lambda: pl.semaphore_wait(ready.at[1], 2))
+            send_head(2 * way - 1, chip * 2, way).start()
+            send_head(2 * way, chip * 2 + 1, way).start()
 
     for q in range(1, half):
         send_x(half + q).start()
@@ -496,7 +522,8 @@
         send_x(q).start()
         send_y(half + q).start()
 
-    recv_head(pn)
+    recv_heads(c, 0)
+    pl.when(g < grp - 1)(lambda: pl.semaphore_wait(ready.at[0], 1))
     share(c)
     for j in range(BPG):
         rspan = slice(j * pair, (j + 1) * pair)
@@ -512,43 +539,69 @@
 
     quarter = rows // 2
     units = [
-        [(c, 0, 0), (c, 0, quarter), (c, 1, 0), (c, 1, quarter)],
-        [(cx, 0, quarter), (cx, 1, quarter), (cy, 0, 0), (cy, 1, 0)],
-        [(cx, 0, 0), (cx, 1, 0), (cy, 0, quarter), (cy, 1, quarter)],
-        [(cd, 0, 0), (cd, 0, quarter), (cd, 1, 0), (cd, 1, quarter)],
+        [[(c, 0, 0), (c, 0, quarter), (c, 1, 0), (c, 1, quarter)]],
+        [[(cx, 0, quarter), (cx, 1, quarter), (cy, 0, 0), (cy, 1, 0)]],
+        [[(cx, 0, 0), (cx, 1, 0), (cy, 0, quarter), (cy, 1, quarter)]],
+        [[(cd, 0, 0), (cd, 0, quarter), (cd, 1, 0), (cd, 1, quarter)]],
     ]
 
-    def seg_rows(ref, seg):
+    def seg_size(u):
+        return quarter // len(units[u])
+
+    def seg_rows(ref, seg, count):
         chip, core, off = seg
-        return ref[pl.ds(pl.multiple_of(chip * pair + core * rows + off, quarter), quarter), :]
-
-    def project(u):
-        segs = units[u]
-        x = jnp.concatenate([toks[chip * 2 + core, off : off + quarter] for chip, core, off in segs], axis=0)
-        cosine = jnp.concatenate([seg_rows(cos_ref, seg) for seg in segs], axis=0)
-        sine = jnp.concatenate([seg_rows(sin_ref, seg) for seg in segs], axis=0)
+        return ref[pl.ds(pl.multiple_of(chip * pair + core * rows + off, count), count), :]
+
+    def run(*tasks):
+        tasks = list(tasks)
+        while tasks:
+            for task in list(tasks):
+                try:
+                    next(task)
+                except StopIteration:
+                    tasks.remove(task)
+
+    def project(u, part):
+        segs, count = units[u][part], seg_size(u)
+        size = 4 * count
+        x = jnp.concatenate([toks[chip * 2 + core, off : off + count] for chip, core, off in segs], axis=0)
+        cosine = jnp.concatenate([seg_rows(cos_ref, seg, count) for seg in segs], axis=0)
+        sine = jnp.concatenate([seg_rows(sin_ref, seg, count) for seg in segs], axis=0)
         qf = jnp.dot(x, wq[...], preferred_element_type=jnp.float32)
+        yield
         qr = rotate_heads(qf, cosine, sine) * HEAD_SIZE**-0.5
         hidden = jnp.concatenate([
             jnp.broadcast_to(
-                jnp.where(block_place > places[g * BPG + chip], neg_large, 0.0), (quarter, LANES)
+                jnp.where(block_place > places[g * BPG + chip], neg_large, 0.0), (count, LANES)
             )
             for chip, _, _ in segs
         ], axis=0)
-        lower = lax.broadcasted_iota(jnp.int32, (pair, LANES), 1) < HEAD_SIZE
+        lower = lax.broadcasted_iota(jnp.int32, (size, LANES), 1) < HEAD_SIZE
         for h in range(qheads):
             v = qr[:, h // 2 * LANES : (h // 2 + 1) * LANES]
             if h % 2:
                 v = pltpu.roll(v, HEAD_SIZE, 1)
-            qs[u, h * pair : (h + 1) * pair, :] = jnp.where(lower, v, hidden).astype(jnp.bfloat16)
-
-    def query_places(u):
-        lane = lax.broadcasted_iota(jnp.int32, (1, pair), 1)
-        place = jnp.zeros((1, pair), jnp.int32)
-        for i, (chip, core, off) in enumerate(units[u]):
+            base = (part * qheads + h) * size
+            qs[u, base : base + size, :] = jnp.where(lower, v, hidden).astype(jnp.bfloat16)
+            yield
+
+    def query_places(u, part):
+        count = seg_size(u)
+        size = 4 * count
+        row = lax.broadcasted_iota(jnp.int32, (1, qheads * size), 1) % size
+        place = jnp.zeros(row.shape, jnp.int32)
+        for i, (chip, core, off) in enumerate(units[u][part]):
             base = places[g * BPG + chip] * pair + core * rows + off
-            place = jnp.where(lane // quarter == i, base + lane % quarter, place)
+            place = jnp.where(row // count == i, base + row % count, place)
         return place
+
+    def sink_row(u):
+        size = 4 * seg_size(u)
+        head = lax.broadcasted_iota(jnp.int32, (1, qheads * size), 1) // size
+        row = jnp.full(head.shape, sinks[s * qheads], jnp.float32)
+        for h in range(1, qheads):
+            row = jnp.where(head == h, sinks[s * qheads + h], row)
+        return row
 
     def prepare(k):
         group = g if k == 0 else others[k - 1]
@@ -560,93 +613,105 @@
             kaug[span, :] = jnp.where(lane < HEAD_SIZE, kv, mark)
             vt[:, span] = jnp.transpose(kv)[HEAD_SIZE:]
 
-    sink_row = jnp.concatenate(
-        [jnp.full((1, pair), sinks[s * qheads + h], jnp.float32) for h in range(qheads)], axis=1
-    )
-    tops = [sink_row for _ in units]
-
-    def part_scores(u, k):
+    tops = [[sink_row(u) for _ in units[u]] for u in range(len(units))]
+
+    def joined(rows_of):
+        return rows_of[0] if len(rows_of) == 1 else jnp.concatenate(rows_of, axis=1)
+
+    floors = [joined(tops[u]) for u in range(len(units))]
+
+    def part_scores(u, k, part):
+        width_of = qheads * 4 * seg_size(u)
+        side = slice(part * width_of, (part + 1) * width_of)
         for j in range(0, chips, 2):
             span = slice(k * group_rows + j * pair, k * group_rows + (j + 2) * pair)
-            part = lax.dot_general(
-                kaug[span, :], qs[u], (((1,), (1,)), ((), ())), preferred_element_type=jnp.float32
+            piece = lax.dot_general(
+                kaug[span, :], qs[u, side, :], (((1,), (1,)), ((), ())), preferred_element_type=jnp.float32
             )
             if k == 0:
-                seen = kpos[j * pair : (j + 2) * pair, :] <= query_places(u)
-                part = jnp.where(jnp.concatenate([seen] * qheads, axis=1), part, neg_large)
-            yield span, part
+                seen = jnp.concatenate([kpos[j * pair : (j + 2) * pair, :]] * (width_of // LANES), axis=1)
+                piece = jnp.where(seen <= query_places(u, part), piece, neg_large)
+            sbuf[u, span, side] = piece
+            tops[u][part] = jnp.maximum(tops[u][part], jnp.max(piece, axis=0, keepdims=True))
+            yield
 
     def score(u, k):
-        for span, part in part_scores(u, k):
-            sbuf[u, span, :] = part
-            tops[u] = jnp.maximum(tops[u], jnp.max(part, axis=0, keepdims=True))
+        for part in range(len(units[u])):
+            yield from part_scores(u, k, part)
 
     bases = [None for _ in units]
     totals = [None for _ in units]
 
-    def absorb(us, stored, fresh, final=False):
+    def absorb(u, stored, fresh, final=False):
         low_key = min(stored + fresh) * group_rows
         high_key = (max(stored + fresh) + 1) * group_rows
-        parts = {u: [piece for k in fresh for piece in part_scores(u, k)] for u in us}
-        factor, mix = {}, {}
-        for u in us:
-            for _, part in parts[u]:
-                tops[u] = jnp.maximum(tops[u], jnp.max(part, axis=0, keepdims=True))
-            if bases[u] is None:
-                total = jnp.exp(sink_row - tops[u])
-            else:
-                factor[u] = jnp.exp(bases[u] - tops[u])
-                total = totals[u] * factor[u]
-            for k in stored:
-                for j in range(0, chips, 2):
-                    span = slice(k * group_rows + j * pair, k * group_rows + (j + 2) * pair)
-                    weights = jnp.exp(sbuf[u, span, :] - tops[u])
-                    pbuf[u, span, :] = weights.astype(jnp.bfloat16)
-                    total = total + jnp.sum(weights, axis=0, keepdims=True)
-            for span, part in parts[u]:
-                weights = jnp.exp(part - tops[u])
-                pbuf[u, span, :] = weights.astype(jnp.bfloat16)
-                total = total + jnp.sum(weights, axis=0, keepdims=True)
-            totals[u], bases[u] = total, tops[u]
-        for u in us:
-            mix[u] = jnp.dot(
-                vt[:, low_key:high_key], pbuf[u, low_key:high_key, :], preferred_element_type=jnp.float32
-            )
-        for u in us:
-            full = mix[u] + mbuf[u] * factor[u] if u in factor else mix[u]
-            if not final:
-                mbuf[u] = full
+        for k in fresh:
+            yield from score(u, k)
+        top = joined(tops[u])
+        factor = None
+        if bases[u] is None:
+            total = jnp.exp(floors[u] - top)
+        else:
+            factor = jnp.exp(bases[u] - top)
+            total = totals[u] * factor
+        for j in range(low_key, high_key, 2 * pair):
+            weights = jnp.exp(sbuf[u, j : j + 2 * pair, :] - top)
+            pbuf[u, j : j + 2 * pair, :] = weights.astype(jnp.bfloat16)
+            total = total + jnp.sum(weights, axis=0, keepdims=True)
+            yield
+        totals[u], bases[u] = total, top
+        mix = jnp.dot(
+            vt[:, low_key:high_key], pbuf[u, low_key:high_key, :], preferred_element_type=jnp.float32
+        )
+        yield
+        if factor is not None:
+            mix = mix + mbuf[u] * factor
+        if not final:
+            mbuf[u] = mix
+            return
+        mix = mix / total
+        count = seg_size(u)
+        size = 4 * count
+        for part in range(len(units[u])):
+            tiles = []
+            for h in range(0, qheads, LANES // size):
+                base = (part * qheads + h) * size
+                tile = jnp.transpose(mix[:, base : base + LANES])
+                tiles.extend(tile[i : i + size] for i in range(0, LANES, size))
+            att = jnp.concatenate(tiles, axis=1).astype(jnp.bfloat16)
+            if len(units[u]) == 1:
+                abuf[u] = att
                 continue
-            full = full / totals[u]
-            heads = [jnp.transpose(full[:, h * pair : (h + 1) * pair]) for h in range(qheads)]
-            abuf[u] = jnp.concatenate(heads, axis=1).astype(jnp.bfloat16)
-        if final:
-            for u in us:
-                ship(u)
+            for i, (_, core, off) in enumerate(units[u][part]):
+                abuf[u, core * rows + off : core * rows + off + count, :] = att[i * count : (i + 1) * count]
+
+    def chain(*tasks):
+        for task in tasks:
+            yield from task
 
     def send_out(u, i):
-        chip, core, off = units[u][i]
+        chip, core, off = (cd, i // 2, 0) if u == 3 else units[u][0][i]
         count = rows if u in (0, 3) else quarter
         src = abuf.at[u, pl.ds(i * quarter, count)]
         dst = obuf.at[pl.ds(off, count), pl.ds(pl.multiple_of(s * qc, qc), qc)]
         return pltpu.make_async_remote_copy(
-            src_ref=src, dst_ref=dst, send_sem=osend.at[u, i],
-            recv_sem=orecv.at[s, u // 2], device_id={"sp": chip * 2 + core},
+            src_ref=src, dst_ref=dst, send_sem=osend.at[0],
+            recv_sem=orecv.at[0], device_id={"sp": chip * 2 + core},
         )
 
     def send_out_partner():
         src = abuf.at[0, pl.ds(pl.multiple_of((1 - p) * rows, rows), rows)]
         dst = obuf.at[:, pl.ds(pl.multiple_of(s * qc, qc), qc)]
         return pltpu.make_async_remote_copy(
-            src_ref=src, dst_ref=dst, send_sem=osend.at[0, 0],
-            recv_sem=orecv.at[s, 0], device_id={"sp": pn},
-        )
-
-    def recv_out(src, off, count, part):
-        dst = obuf.at[pl.ds(off, count), pl.ds(pl.multiple_of(src * qc, qc), qc)]
+            src_ref=src, dst_ref=dst, send_sem=osend.at[0],
+            recv_sem=orecv.at[0], device_id={"sp": pn},
+        )
+
+    def wait_out(sem):
+        span = pl.ds(0, (sp - 1) * qc)
         pltpu.make_async_remote_copy(
-            src_ref=abuf.at[0, pl.ds(0, count)], dst_ref=dst, send_sem=osend.at[0, 0],
-            recv_sem=orecv.at[src, part], device_id={"sp": src},
+            src_ref=obuf.at[:, span], dst_ref=obuf.at[:, span], send_sem=sem, recv_sem=sem,
+            device_id={"sp": pn},
         ).wait_recv()
 
     def ship(u):
@@ -664,112 +729,90 @@
 
     def stage(k):
         qx, qy = (k + half) % pieces, k
-        forward(0, qx).wait_recv()
+        arrived(0, qx)
         if k < half:
             relay(qx).start()
-        forward(0, qx).start()
-        forward(1, qy).wait_recv()
+        forward(0, qx, k // half).start()
+        arrived(1, qy)
         if k < half:
             relay(qy).start()
-        forward(1, qy).start()
-
-    def stage_partner(k):
-        qx, qy = (k + half) % pieces, k
-        send_piece(cx * 2 + 1 - p, qx, pn, fsend.at[0, qx]).wait_recv()
-        send_piece(cy * 2 + 1 - p, qy, pn, fsend.at[1, qy]).wait_recv()
+        forward(1, qy, k // half).start()
 
     def stage_far(q):
         for r in (q, q + half):
-            forward(2, r).wait_recv()
-            forward(2, r).start()
-
-    def stage_far_partner(q):
-        for r in (q, q + half):
-            send_piece(cd * 2 + 1 - p, r, pn, fsend.at[2, r]).wait_recv()
-
-    send_own(pn, pn).wait_recv()
+            arrived(2, r)
+            forward(2, r, 2).start()
+
+    def partner(i):
+        wait_rows(drecv.at[i], 1)
+
+    stage(0)
+    partner(3)
     wq_copy.wait()
-    project(0)
-    stage(0)
-    for chip in (cx, cy, cd):
-        recv_head(chip * 2)
-        recv_head(chip * 2 + 1)
+    run(project(0, 0))
+    for chip, way in ((cx, 2), (cy, 3), (cd, 1)):
+        recv_heads(chip, way)
         share(chip)
+    near, rest = (c,), (cx, cy, cd)
+    pl.when(inner)(lambda: recv_group(0, near))
     prepare(0)
-    score(0, 0)
+    run(score(0, 0))
+    pl.when(inner)(lambda: recv_group(1, near))
     stage(1)
-    for k in range(half):
-        stage_partner(k)
-    project(1)
-    score(1, 0)
-    recv_group(0)
-    pl.when(inner)(lambda: recv_group(1))
+    partner(0)
+    run(project(1, 0))
+    run(score(1, 0))
+    pl.when(outer)(lambda: recv_group(0, near))
+    recv_group(0, rest)
+
+    @pl.when(inner)
+    def _():
+        recv_group(1, rest)
+        recv_group(2, near)
+
+    stage(2)
     prepare(1)
-    score(0, 1)
-    score(1, 1)
-    stage(2)
-    absorb((0, 1), [0, 1], [])
+    run(score(0, 1), score(1, 1))
     stage(3)
-    for k in range(half, pieces):
-        stage_partner(k)
-    project(2)
-    score(2, 0)
-    score(2, 1)
-    pl.when(jnp.logical_not(inner))(lambda: recv_group(1))
-    pl.when(inner)(lambda: recv_group(2))
+    partner(1)
+    run(chain(project(2, 0), score(2, 0), score(2, 1)), chain(absorb(0, [0, 1], []), absorb(1, [0, 1], [])))
+    pl.when(outer)(lambda: recv_group(1, near + rest))
+    pl.when(inner)(lambda: recv_group(2, rest))
     stage_far(0)
     prepare(2)
-    absorb((0, 1), [], [2])
+    run(absorb(0, [], [2]), absorb(1, [], [2]), score(2, 2))
     stage_far(1)
-    absorb((2,), [0, 1], [2])
-    for q in range(half):
-        stage_far_partner(q)
-    project(3)
-    for k in range(grp - 1):
-        score(3, k)
-    pl.when(jnp.logical_not(inner))(lambda: recv_group(2))
+    run(absorb(2, [0, 1, 2], []))
+    partner(2)
+    run(chain(project(3, 0), score(3, 0), score(3, 1), score(3, 2), absorb(3, [0, 1, 2], [])))
+    pl.when(outer)(lambda: recv_group(2, near + rest))
     prepare(3)
-    absorb((3,), [0, 1, 2], [3], True)
-    absorb((1, 2), [], [3], True)
-    absorb((0,), [], [3], True)
-
-    recv_out(pn, 0, rows, 0)
-    for core in range(2):
-        recv_out(cx * 2 + core, quarter, quarter, 0)
-        recv_out(cy * 2 + core, 0, quarter, 0)
-        recv_out(cx * 2 + core, 0, quarter, 1)
-        recv_out(cy * 2 + core, quarter, quarter, 1)
-        recv_out(cd * 2 + core, 0, rows, 1)
+    run(absorb(3, [], [3], True), absorb(1, [], [3], True))
+    ship(3)
+    ship(1)
+    run(absorb(2, [], [3], True), absorb(0, [], [3], True))
+    ship(2)
+    ship(0)
+
+    wait_out(orecv.at[0])
     out[...] = obuf[...]
-    send_own(s, pn).wait_send()
-    for q in range(pieces):
-        send_x(q).wait_send()
-        send_y(q).wait_send()
-        relay(q).wait_send()
-        for k in range(3):
-            forward(k, q).wait_send()
-    for i in range(sp - 1):
-        send_head(i, pn).wait_send()
-    for chip in range(chips):
-        @pl.when(g > 0)
-        def _():
-            send_chunk(g, chip, g - 1, 1).wait_send()
-
-        @pl.when(g < grp - 1)
-        def _():
-            send_chunk(g, chip, g + 1, 0).wait_send()
-
-        @pl.when(inner)
-        def _():
-            for k in range(3):
-                pass_on(k, chip).wait_send()
-
-    send_out_partner().wait_send()
-    for i in range(4):
-        send_out(1, i).wait_send()
-        send_out(2, i).wait_send()
-    send_out(3, 0).wait_send()
-    send_out(3, 2).wait_send()
+    wait_rows(tsend.at[0], sp - 1)
+    kept = kvo.at[pl.ds(0, sp - 1)]
+    pltpu.make_async_remote_copy(
+        src_ref=kept, dst_ref=kept, send_sem=ksend.at[0], recv_sem=ksend.at[0], device_id={"sp": pn}
+    ).wait_recv()
+
+    def wait_keys(way, count):
+        span = pl.ds(0, count)
+        pltpu.make_async_remote_copy(
+            src_ref=kvb.at[span], dst_ref=kvb.at[span], send_sem=zsend.at[way],
+            recv_sem=zsend.at[way], device_id={"grp": g},
+        ).wait_recv()
+
+    pl.when(g > 0)(lambda: wait_keys(1, group_rows))
+    pl.when(g < grp - 1)(lambda: wait_keys(0, group_rows))
+    pl.when(inner)(lambda: wait_keys(2, 3 * group_rows))
+    wait_out(osend.at[0])
 
 
 def per_plane(tokens, query_weight, key_value_weight, block_places, sinks):
@@ -786,7 +829,7 @@
     hbm = pl.BlockSpec(memory_space=pl.ANY)
     dma = pltpu.SemaphoreType.DMA
     bf16, f32 = jnp.bfloat16, jnp.float32
-    return pl.pallas_call(
+    result = pl.pallas_call(
         functools.partial(plane_kernel, grp, sp, qheads),
         out_shape=pltpu.VMEM((rows, qc * sp), bf16),
         in_specs=[hbm] * 5,
@@ -810,24 +853,39 @@
             pltpu.VMEM((group_rows, LANES), f32),
             pltpu.VMEM((group_rows, LANES), f32),
             pltpu.VMEM((group_rows, LANES), jnp.int32),
-            dma((4 + sp,)),
-            dma((pieces,)),
-            dma((pieces,)),
+            dma((6,)),
             dma((1,)),
-            dma((pieces,)),
             dma((3, pieces)),
-            dma((sp, pieces)),
-            dma((sp,)),
-            dma((sp,)),
-            dma((5, sp // 2)),
+            dma((5,)),
+            dma((1,)),
+            dma((sp // 2,)),
+            dma((3,)),
             dma((grp, sp // 2)),
-            dma((4, 4)),
-            dma((sp, 2)),
+            dma((1,)),
+            dma((1,)),
+            pltpu.SemaphoreType.REGULAR((2,)),
         ],
         compiler_params=pltpu.CompilerParams(
             has_side_effects=True, collective_id=0, vmem_limit_bytes=60 * 1024 * 1024
         ),
     )(tokens, query_weight, key_value_weight, block_places, sinks)
+    return result
+
+
+def write_out(result, out, sem):
+    copy = pltpu.make_async_copy(result, out, sem)
+    copy.start()
+    copy.wait()
+
+
+def written(result):
+    return pl.pallas_call(
+        write_out,
+        out_shape=jax.ShapeDtypeStruct(result.shape, result.dtype),
+        in_specs=[pl.BlockSpec(memory_space=pltpu.VMEM)],
+        out_specs=pl.BlockSpec(memory_space=pl.ANY),
+        scratch_shapes=[pltpu.SemaphoreType.DMA],
+    )(result)
 
 
 def local_form(tokens, query_weight, key_value_weight, block_places, sinks):

time: 32.5 us -> 30 us (0.923)
  Pallas kernels: 31.7 us -> 29.2 us
    pallas_call x1, Pallas kernels: 31.7 us -> 29.2 us  [per_plane(): pl.pallas_call(functools.partial(plane_kernel, grp, sp, qheads), out_shap...]
where the time goes in v3:
time: 30 us; the launch traced here: 29.9 us
  Pallas kernels  29.2 us (97%)
  local copies, waits for them, and re-layouts  0.71 us (2%)
    pallas_call x1, Pallas kernels, per_plane(): pl.pallas_call(functools.partial(plane_kernel, grp, sp, qheads), out_shap...  29.2 us
    unnamed x1, local copies, waits for them, and re-layouts  0.71 us

profile of v3, /device:TPU:0, one launch (start us, length us, event | category | flops | bytes accessed | tf_op | source)
XLA Modules:
  0.0 29.9 jit_solution(364671811312486301)
XLA Ops:
  0.0 29.2 %shard_map.55 = bf16[64,2048]{1,0:T(8,128)(2,1)S(1)} custom-call(bf16[64,2880]{1,0:T(8,128)(2,1)} %tok_any.1, bf16[2880,256]{1,0:T(8,128)(2,1)} %wq_any.1, bf16[2880,1024]{1,0:T(8,128)(2,1)} %kvw_any.1, s32[16]{0:T(128)} %places_any.1, f32[32]{0:T(128)} %sinks_any.1), custom_call_target="tpu_custom_call" | custom-call | tf_op jit(solution)/shard_map/pallas_call | solution.py:832
  29.2 0.7 %copy.7 = bf16[64,2048]{1,0:T(8,128)(2,1)} copy(bf16[64,2048]{1,0:T(8,128)(2,1)S(1)} %shard_map.55) | data formatting | bytes 524288

commit v4 on v3

--- a/solution.py
+++ b/solution.py
@@ -623,15 +623,17 @@
     def part_scores(u, k, part):
         width_of = qheads * 4 * seg_size(u)
         side = slice(part * width_of, (part + 1) * width_of)
-        for j in range(0, chips, 2):
-            span = slice(k * group_rows + j * pair, k * group_rows + (j + 2) * pair)
-            piece = lax.dot_general(
-                kaug[span, :], qs[u, side, :], (((1,), (1,)), ((), ())), preferred_element_type=jnp.float32
-            )
+        span = slice(k * group_rows, (k + 1) * group_rows)
+        whole = lax.dot_general(
+            kaug[span, :], qs[u, side, :], (((1,), (1,)), ((), ())), preferred_element_type=jnp.float32
+        )
+        yield
+        for j in range(0, group_rows, pair):
+            piece = whole[j : j + pair, :]
             if k == 0:
-                seen = jnp.concatenate([kpos[j * pair : (j + 2) * pair, :]] * (width_of // LANES), axis=1)
+                seen = jnp.concatenate([kpos[j : j + pair, :]] * (width_of // LANES), axis=1)
                 piece = jnp.where(seen <= query_places(u, part), piece, neg_large)
-            sbuf[u, span, side] = piece
+            sbuf[u, k * group_rows + j : k * group_rows + j + pair, side] = piece
             tops[u][part] = jnp.maximum(tops[u][part], jnp.max(piece, axis=0, keepdims=True))
             yield
 
@@ -779,19 +781,21 @@
     pl.when(outer)(lambda: recv_group(1, near + rest))
     pl.when(inner)(lambda: recv_group(2, rest))
     stage_far(0)
+    pl.when(p == 1)(lambda: stage_far(1))
     prepare(2)
     run(absorb(0, [], [2]), absorb(1, [], [2]), score(2, 2))
-    stage_far(1)
+    pl.when(p == 0)(lambda: stage_far(1))
     run(absorb(2, [0, 1, 2], []))
     partner(2)
     run(chain(project(3, 0), score(3, 0), score(3, 1), score(3, 2), absorb(3, [0, 1, 2], [])))
     pl.when(outer)(lambda: recv_group(2, near + rest))
     prepare(3)
-    run(absorb(3, [], [3], True), absorb(1, [], [3], True))
+    run(absorb(3, [], [3], True))
     ship(3)
+    run(absorb(1, [], [3], True), absorb(2, [], [3], True))
     ship(1)
-    run(absorb(2, [], [3], True), absorb(0, [], [3], True))
     ship(2)
+    run(absorb(0, [], [3], True))
     ship(0)
 
     wait_out(orecv.at[0])

time: 30 us -> 29.7 us (0.990)
  Pallas kernels: 29.2 us -> 28.9 us
    pallas_call x1, Pallas kernels: 29.2 us -> 28.9 us  [per_plane(): pl.pallas_call(functools.partial(plane_kernel, grp, sp, qheads), out_shap...]
where the time goes in v4:
time: 29.7 us; the launch traced here: 29.6 us
  Pallas kernels  28.9 us (97%)
  local copies, waits for them, and re-layouts  0.71 us (2%)
    pallas_call x1, Pallas kernels, per_plane(): pl.pallas_call(functools.partial(plane_kernel, grp, sp, qheads), out_shap...  28.9 us
    unnamed x1, local copies, waits for them, and re-layouts  0.71 us

profile of v4, /device:TPU:0, one launch (start us, length us, event | category | flops | bytes accessed | tf_op | source)
XLA Modules:
  0.0 29.6 jit_solution(2567413279152533559)
XLA Ops:
  0.0 28.9 %shard_map.55 = bf16[64,2048]{1,0:T(8,128)(2,1)S(1)} custom-call(bf16[64,2880]{1,0:T(8,128)(2,1)} %tok_any.1, bf16[2880,256]{1,0:T(8,128)(2,1)} %wq_any.1, bf16[2880,1024]{1,0:T(8,128)(2,1)} %kvw_any.1, s32[16]{0:T(128)} %places_any.1, f32[32]{0:T(128)} %sinks_any.1), custom_call_target="tpu_custom_call" | custom-call | tf_op jit(solution)/shard_map/pallas_call | solution.py:836
  28.9 0.7 %copy.7 = bf16[64,2048]{1,0:T(8,128)(2,1)} copy(bf16[64,2048]{1,0:T(8,128)(2,1)S(1)} %shard_map.55) | data formatting | bytes 524288

commit v5 on v4

--- a/solution.py
+++ b/solution.py
@@ -777,13 +777,15 @@
     run(score(0, 1), score(1, 1))
     stage(3)
     partner(1)
-    run(chain(project(2, 0), score(2, 0), score(2, 1)), chain(absorb(0, [0, 1], []), absorb(1, [0, 1], [])))
+    run(chain(project(2, 0), score(2, 0)), absorb(1, [0, 1], []))
+    pl.when(inner)(lambda: recv_group(2, (cx,)))
+    run(score(2, 1))
     pl.when(outer)(lambda: recv_group(1, near + rest))
-    pl.when(inner)(lambda: recv_group(2, rest))
+    pl.when(inner)(lambda: recv_group(2, (cy, cd)))
     stage_far(0)
     pl.when(p == 1)(lambda: stage_far(1))
     prepare(2)
-    run(absorb(0, [], [2]), absorb(1, [], [2]), score(2, 2))
+    run(absorb(1, [], [2]), score(0, 2), score(2, 2))
     pl.when(p == 0)(lambda: stage_far(1))
     run(absorb(2, [0, 1, 2], []))
     partner(2)
@@ -795,7 +797,7 @@
     run(absorb(1, [], [3], True), absorb(2, [], [3], True))
     ship(1)
     ship(2)
-    run(absorb(0, [], [3], True))
+    run(absorb(0, [0, 1, 2], [3], True))
     ship(0)
 
     wait_out(orecv.at[0])

time: 29.7 us -> 29.6 us (level)
  no operation moved by 1% of the time
where the time goes in v5:
time: 29.6 us; the launch traced here: 29.5 us
  Pallas kernels  28.8 us (97%)
  local copies, waits for them, and re-layouts  0.71 us (2%)
    pallas_call x1, Pallas kernels, per_plane(): pl.pallas_call(functools.partial(plane_kernel, grp, sp, qheads), out_shap...  28.8 us
    unnamed x1, local copies, waits for them, and re-layouts  0.71 us

profile of v5, /device:TPU:0, one launch (start us, length us, event | category | flops | bytes accessed | tf_op | source)
XLA Modules:
  0.0 29.5 jit_solution(16263479983902134333)
XLA Ops:
  0.0 28.8 %shard_map.55 = bf16[64,2048]{1,0:T(8,128)(2,1)S(1)} custom-call(bf16[64,2880]{1,0:T(8,128)(2,1)} %tok_any.1, bf16[2880,256]{1,0:T(8,128)(2,1)} %wq_any.1, bf16[2880,1024]{1,0:T(8,128)(2,1)} %kvw_any.1, s32[16]{0:T(128)} %places_any.1, f32[32]{0:T(128)} %sinks_any.1), custom_call_target="tpu_custom_call" | custom-call | tf_op jit(solution)/shard_map/pallas_call | solution.py:838
  28.8 0.7 %copy.7 = bf16[64,2048]{1,0:T(8,128)(2,1)} copy(bf16[64,2048]{1,0:T(8,128)(2,1)S(1)} %shard_map.55) | data formatting | bytes 524288

commit v6 on v5

--- a/solution.py
+++ b/solution.py
@@ -351,13 +351,25 @@
                     wsem.at[2 + k // 2],
                 )
             )
-    tok_copy = pltpu.make_async_copy(tok_any, toks.at[s], wsem.at[0])
+    def load_piece(q, sem):
+        span = pl.ds(q * piece_rows, piece_rows)
+        return pltpu.make_async_copy(tok_any.at[span], toks.at[s, span], wsem.at[sem])
+
+    def wait_pieces(sem, count):
+        span = pl.ds(0, count * piece_rows)
+        pltpu.make_async_copy(tok_any.at[span], toks.at[s, span], wsem.at[sem]).wait()
+
+    first_pieces = (half, 0)
+    other_pieces = [q for q in range(pieces) if q not in first_pieces]
     wq_copy = pltpu.make_async_copy(wq_any, wq, wsem.at[1])
     pcopy = pltpu.make_async_copy(places_any, places, wsem.at[4])
     scopy = pltpu.make_async_copy(sinks_any, sinks, wsem.at[5])
     pcopy.start()
     scopy.start()
-    tok_copy.start()
+    for q in first_pieces:
+        load_piece(q, 0).start()
+    for q in other_pieces:
+        load_piece(q, 6).start()
     for copy in wcopies:
         copy.start()
     wq_copy.start()
@@ -472,11 +484,12 @@
     own_place = places[g * BPG + c] * pair + p * rows + lax.broadcasted_iota(jnp.int32, (rows, LANES), 0)
     own_angles = own_place.astype(jnp.float32) * inverse
     own_cos, own_sin = jnp.cos(own_angles), jnp.sin(own_angles) * sign
-    tok_copy.wait()
+    wait_pieces(0, 2)
     pl.semaphore_wait(barrier, 5 + jnp.minimum(g, 1) + 2 * (c // (chips // 2)))
-    send_own(s, pn).start()
     send_x(half).start()
     send_y(0).start()
+    wait_pieces(6, pieces - 2)
+    send_own(s, pn).start()
 
     @pl.when(g > 0)
     def _():
@@ -859,10 +872,10 @@
             pltpu.VMEM((group_rows, LANES), f32),
             pltpu.VMEM((group_rows, LANES), f32),
             pltpu.VMEM((group_rows, LANES), jnp.int32),
-            dma((6,)),
+            dma((7,)),
             dma((1,)),
             dma((3, pieces)),
-            dma((5,)),
+            dma((4,)),
             dma((1,)),
             dma((sp // 2,)),
             dma((3,)),

time: 29.6 us -> 29.6 us (level)
  no operation moved by 1% of the time
where the time goes in v6:
time: 29.6 us; the launch traced here: 29.5 us
  Pallas kernels  28.8 us (97%)
  local copies, waits for them, and re-layouts  0.71 us (2%)
    pallas_call x1, Pallas kernels, per_plane(): pl.pallas_call(functools.partial(plane_kernel, grp, sp, qheads), out_shap...  28.8 us
    unnamed x1, local copies, waits for them, and re-layouts  0.71 us

profile of v6, /device:TPU:0, one launch (start us, length us, event | category | flops | bytes accessed | tf_op | source)
XLA Modules:
  0.0 29.5 jit_solution(2189396037683593779)
XLA Ops:
  0.0 28.8 %shard_map.55 = bf16[64,2048]{1,0:T(8,128)(2,1)S(1)} custom-call(bf16[64,2880]{1,0:T(8,128)(2,1)} %tok_any.1, bf16[2880,256]{1,0:T(8,128)(2,1)} %wq_any.1, bf16[2880,1024]{1,0:T(8,128)(2,1)} %kvw_any.1, s32[16]{0:T(128)} %places_any.1, f32[32]{0:T(128)} %sinks_any.1), custom_call_target="tpu_custom_call" | custom-call | tf_op jit(solution)/shard_map/pallas_call | solution.py:851
  28.8 0.7 %copy.7 = bf16[64,2048]{1,0:T(8,128)(2,1)} copy(bf16[64,2048]{1,0:T(8,128)(2,1)S(1)} %shard_map.55) | data formatting | bytes 524288
